TPU v7x, 32 devices: a whole 2x2x4 slice. The times are simulated.
32 devices in a mesh: crop: 2 (over x), seq: 2 (over y), res: 8 (over z, core).
Axes of the slice: x: 2, y: 2, z: 4, core: 2. Of those that a mesh axis runs over, the one named last changes fastest.
Arguments:
- aligned_chain_embedding: bfloat16 [128, 32, 256], P(('crop', 'seq'), 'res'), parts along dimension 0, may hold values from -6 to 6
- alignment_mask: int32 [128, 32], P(('crop', 'seq'), 'res'), parts along dimension 0, may hold values from 0 to 1, as said below
- resolved_residue_mask: int32 [64], P('crop'), parts along dimension 0, may hold values 0 or 1
- pairwise_state: bfloat16 [64, 32, 128], P(('crop', 'seq'), 'res'), parts along dimension 0, may hold values from -8 to 8
- combined_projection_matrix: bfloat16 [256, 1024], replicated, may hold values from -0.375 to 0.375
- pair_bias_weight: bfloat16 [128, 8], replicated, may hold values from -8 to 8
- final_projection_matrix: bfloat16 [256, 256], replicated, may hold values from -0.375 to 0.375
- left_right_projection_matrix: bfloat16 [256, 64], replicated, may hold values from -1.5 to 1.5
- outer_mean_weight: bfloat16 [1024, 128], replicated, may hold values from -0.1875 to 0.1875
Outputs:
- alignment_output: bfloat16 [128, 32, 256], P(('crop', 'seq'), 'res'), parts along dimension 0
- pairwise_output: bfloat16 [64, 32, 128], P(('crop', 'seq'), 'res'), parts along dimension 0
There are 2 independent parts, one for each index of `crop`. A program takes and returns all parts, laid end to end along the dimension named above; an argument that names none is the same for every part. Nothing has to cross between parts.
Inputs may be any that keep to these rules, and one draw needn't show every extreme that they name: `alignment_mask`: sequence 0 has no gaps.
All inputs are finite; a program needn't handle non-finite values.
Results may differ from a plain program's by a relative error of at most 0.013.
The roundings to bfloat16 on the way count: a program that leaves them out, or rounds other values in their place, can miss the bound.
Values may be sent and summed in bfloat16 or wider, within the bound.
A program may use at most 64 MiB of HBM per device.

v0:
```python
import functools
import math

import jax
import jax.numpy as jnp
from jax import lax
from jax.experimental import pallas as pl
from jax.experimental.pallas import tpu as pltpu
from jax.sharding import PartitionSpec as P

ROW_FEATURES = 256
CZ = 128
HEAD_NUMBER = 8
PER_HEAD_DIM = 32
PROJ_FEATURES = 32


epsilon = 1e-05


def layer_normalize(values):
    values = values.astype(jnp.float32)
    average = jnp.mean(values, axis=-1, keepdims=True)
    centered = values - average
    variance = jnp.mean(centered * centered, axis=-1, keepdims=True)
    return centered * lax.rsqrt(variance + epsilon)


def outer_rows(left_side, right_side, project):
    row_total = left_side.shape[1]
    col_total = right_side.shape[1]
    block_rows = math.gcd(row_total, max(1, 2048 // col_total))

    def outer_block(start):
        product = jnp.einsum(
            "sic,sje->ijce", left_side, right_side, preferred_element_type=jnp.float32
        )
        flattened = product.reshape(block_rows * col_total, PROJ_FEATURES * PROJ_FEATURES)
        return jnp.dot(flattened, project, precision=lax.Precision.HIGHEST).reshape(
            block_rows, col_total, CZ
        )

    starts = jnp.arange(row_total // block_rows, dtype=jnp.int32) * block_rows
    return lax.map(outer_block, starts).reshape(row_total, col_total, CZ)


def per_device(
    aligned_chain_embedding,
    alignment_mask,
    resolved_residue_mask,
    pairwise_state,
    combined_projection_matrix,
    pair_bias_weight,
    final_projection_matrix,
    left_right_projection_matrix,
    outer_mean_weight,
):
    chain_count = aligned_chain_embedding.shape[0]
    amino_count = aligned_chain_embedding.shape[1]
    res_ranks = lax.axis_size("res")
    seq_groups = lax.axis_size("seq")
    full_length = amino_count * res_ranks
    row_count = full_length // seq_groups
    item_count = HEAD_NUMBER * chain_count // res_ranks
    per_head = min(item_count, chain_count)
    head_count = item_count // per_head
    my_rank = lax.axis_index("res")
    my_group = lax.axis_index("seq")
    standardized_rows = layer_normalize(aligned_chain_embedding).astype(jnp.bfloat16)
    linear_mapped = jnp.dot(
        standardized_rows.reshape(chain_count * amino_count, ROW_FEATURES),
        combined_projection_matrix,
        preferred_element_type=jnp.float32,
    )
    linear_mapped = linear_mapped.reshape(chain_count, amino_count, 4, HEAD_NUMBER, PER_HEAD_DIM)
    queries = (linear_mapped[:, :, 0] * PER_HEAD_DIM ** (-0.5)).astype(jnp.bfloat16)
    key_rows = linear_mapped[:, :, 1].astype(jnp.bfloat16)
    value_rows = linear_mapped[:, :, 2].astype(jnp.bfloat16)
    sigmoid_factor = jax.nn.sigmoid(linear_mapped[:, :, 3])
    stacked = jnp.stack([queries, key_rows, value_rows], axis=2)
    stacked = jnp.transpose(stacked, (3, 0, 1, 2, 4)).reshape(
        HEAD_NUMBER * chain_count, amino_count, 3 * PER_HEAD_DIM
    )
    presence_mask_flags = alignment_mask.astype(jnp.bfloat16)
    key_flags = jnp.broadcast_to(
        presence_mask_flags[None], (HEAD_NUMBER, chain_count, amino_count)
    ).reshape(HEAD_NUMBER * chain_count, amino_count)
    arrived, arrived_flags = (
        lax.all_to_all(stacked, "res", split_axis=0, concat_axis=1, tiled=True),
        lax.all_to_all(key_flags, "res", split_axis=0, concat_axis=1, tiled=True),
    )
    pair_normed = layer_normalize(pairwise_state).astype(jnp.bfloat16)
    local_bias = jnp.dot(
        pair_normed.reshape(row_count * amino_count, CZ),
        pair_bias_weight,
        preferred_element_type=jnp.float32,
    )
    local_bias = jnp.transpose(
        local_bias.astype(jnp.bfloat16).reshape(row_count, amino_count, HEAD_NUMBER), (2, 0, 1)
    )
    bias_cols = lax.all_gather(local_bias, "res", axis=2, tiled=True)
    whole_bias = lax.all_gather(bias_cols, "seq", axis=1, tiled=True)
    first_head = my_rank * item_count // chain_count
    head_bias = lax.dynamic_slice_in_dim(whole_bias, first_head, head_count, 0)
    grouped = arrived.reshape(head_count, per_head, full_length, 3, PER_HEAD_DIM)
    key_validity_mask = (
        arrived_flags.reshape(head_count, per_head, full_length).astype(jnp.float32) - 1.0
    ) * 1000000000.0
    scores = jnp.einsum(
        "gpid,gpjd->gpij",
        grouped[:, :, :, 0],
        grouped[:, :, :, 1],
        preferred_element_type=jnp.float32,
    )
    scores = scores + head_bias.astype(jnp.float32)[:, None] + key_validity_mask[:, :, None, :]
    row_max = jnp.max(scores, axis=-1, keepdims=True)
    exponent = jnp.exp(scores - row_max)
    weights = (exponent / jnp.sum(exponent, axis=-1, keepdims=True)).astype(jnp.bfloat16)
    softmax_mixed = jnp.einsum(
        "gpij,gpjd->gpid", weights, grouped[:, :, :, 2], preferred_element_type=jnp.float32
    )
    softmax_mixed = softmax_mixed.astype(jnp.bfloat16).reshape(
        item_count, full_length, PER_HEAD_DIM
    )
    returned = lax.all_to_all(softmax_mixed, "res", split_axis=1, concat_axis=0, tiled=True)
    returned = jnp.transpose(
        returned.reshape(HEAD_NUMBER, chain_count, amino_count, PER_HEAD_DIM), (1, 2, 0, 3)
    )
    sigmoid_scaled = (
        (sigmoid_factor * returned.astype(jnp.float32))
        .astype(jnp.bfloat16)
        .reshape(chain_count * amino_count, ROW_FEATURES)
    )
    embedding_increment = jnp.dot(
        sigmoid_scaled, final_projection_matrix, preferred_element_type=jnp.float32
    ).reshape(chain_count, amino_count, ROW_FEATURES)
    alignment_output = (aligned_chain_embedding.astype(jnp.float32) + embedding_increment).astype(
        jnp.bfloat16
    )
    standardized_product = layer_normalize(alignment_output).astype(jnp.bfloat16)
    left_right_vectors = jnp.dot(
        standardized_product.reshape(chain_count * amino_count, ROW_FEATURES),
        left_right_projection_matrix,
        preferred_element_type=jnp.float32,
    )
    left_right_vectors = left_right_vectors.reshape(chain_count, amino_count, 2, PROJ_FEATURES)
    entry_present = alignment_mask.astype(jnp.float32)[:, :, None]
    left_side = (left_right_vectors[:, :, 0] * entry_present).astype(jnp.bfloat16)
    right_side = (left_right_vectors[:, :, 1] * entry_present).astype(jnp.bfloat16)
    left_all, left_flags = (
        lax.all_gather(left_side, "res", axis=1, tiled=True),
        lax.all_gather(presence_mask_flags, "res", axis=1, tiled=True),
    )
    project = outer_mean_weight.astype(jnp.float32)
    row_start = my_group * row_count
    left_full, flag_full = (
        lax.all_to_all(left_all, "seq", split_axis=1, concat_axis=0, tiled=True),
        lax.all_to_all(left_flags, "seq", split_axis=1, concat_axis=0, tiled=True),
    )
    right_full, right_flags = (
        lax.all_gather(right_side, "seq", axis=0, tiled=True),
        lax.all_gather(presence_mask_flags, "seq", axis=0, tiled=True),
    )
    counts = jnp.dot(flag_full.T, right_flags, preferred_element_type=jnp.float32)
    outer = outer_rows(left_full, right_full, project)
    col_start = my_rank * amino_count
    row_mask = lax.dynamic_slice_in_dim(resolved_residue_mask, row_start, row_count).astype(
        jnp.float32
    )
    col_mask = lax.dynamic_slice_in_dim(resolved_residue_mask, col_start, amino_count).astype(
        jnp.float32
    )
    pair_mask = row_mask[:, None] * col_mask[None, :]
    pairwise_output = (
        pairwise_state.astype(jnp.float32) + pair_mask[:, :, None] * (outer / counts[:, :, None])
    ).astype(jnp.bfloat16)
    return (alignment_output, pairwise_output)


LANES = 128
F32 = jnp.float32
BF16 = jnp.bfloat16


def iota(shape, axis):
    return lax.broadcasted_iota(jnp.int32, shape, axis)


def dot(a, b, ca=1, cb=0):
    return lax.dot_general(a, b, (((ca,), (cb,)), ((), ())), preferred_element_type=F32)


def one_hot(cond):
    return jnp.where(cond, 1.0, 0.0).astype(BF16)


def fused_kernel(
    groups, ranks, chains, aminos,
    emb_ref, mask_ref, resolved_ref, pair_ref, proj_hbm, bias_w_ref, final_hbm, lr_ref, outer_hbm,
    out_ref, pair_out_ref,
    emb_buf, aux_buf, side_send, side_buf, out_send, out_buf,
    product_buf, lhs_buf, proj_ref, final_ref, outer_ref,
    emb_s, emb_r, aux_s, aux_r, side_s, side_r, out_s, out_r, load_s,
):
    devices = groups * ranks
    per = chains // ranks
    tile = per * aminos
    rows = ranks * tile
    full = ranks * aminos
    pair_rows = full // groups
    pairs = pair_rows * aminos
    half = rows // groups
    group = lax.axis_index("seq")
    rank = lax.axis_index("res")
    me = group * ranks + rank

    def peer_of(k):
        peer = lax.rem(me + k, devices)
        return peer, {"seq": peer // ranks, "res": lax.rem(peer, ranks)}

    barrier = pltpu.get_barrier_semaphore()
    for k in range(1, devices):
        pl.semaphore_signal(
            barrier, inc=1, device_id=peer_of(k)[1], device_id_type=pl.DeviceIdType.MESH
        )

    loads = []
    for k, (src, dst) in enumerate(
        ((proj_hbm, proj_ref), (final_hbm, final_ref), (outer_hbm, outer_ref))
    ):
        loads.append(pltpu.make_async_copy(src, dst, load_s.at[k]))
        loads[-1].start()

    def send(src, dst, ssem, rsem, device):
        copy = pltpu.make_async_remote_copy(
            src_ref=src, dst_ref=dst, send_sem=ssem, recv_sem=rsem,
            device_id=device, device_id_type=pl.DeviceIdType.MESH,
        )
        copy.start()
        return copy

    pair_value = pair_ref[...]
    pair_normed = layer_normalize(pair_value).astype(BF16)
    wide = jnp.concatenate([pair_normed] * groups, axis=0)
    wide = jnp.where(iota((groups * pairs, CZ), 0) // pairs == group, wide, jnp.zeros_like(wide))
    own_bias = dot(bias_w_ref[...], wide, 1, 1)
    spread = dot(mask_ref[...].astype(F32).astype(BF16), one_hot(
        iota((chains, LANES), 1) // aminos == iota((chains, LANES), 0)))
    flag_row = jnp.sum(
        jnp.where(iota((aminos, LANES), 1) % aminos == iota((aminos, LANES), 0), spread, 0.0),
        axis=0, keepdims=True)
    flags = jnp.broadcast_to(flag_row, (HEAD_NUMBER, LANES))
    aux_buf[me] = jnp.concatenate([own_bias, flags], axis=0).astype(BF16)
    own = pl.ds(rank * per, per)
    emb_buf[own] = emb_ref[own]

    pl.semaphore_wait(barrier, devices - 1)
    pending = []
    emb_copies = []
    for k in range(1, ranks):
        peer = lax.rem(rank + k, ranks)
        emb_copies.append(send(emb_ref.at[pl.ds(peer * per, per)], emb_buf.at[own],
                               emb_s.at[k], emb_r.at[k],
                               {"seq": group, "res": peer}))
    aux_copies = []
    for k in range(1, devices):
        aux_copies.append(send(aux_buf.at[me], aux_buf.at[me], aux_s.at[k], aux_r.at[k],
                               peer_of(k)[1]))

    quads = pair_rows // aminos

    def row_of(q):
        return (q % quads) * aminos + (q % pair_rows) // quads

    q0 = iota((pairs, pairs), 0)
    q1 = iota((pairs, pairs), 1)
    order = one_hot(row_of(q0) * aminos + q0 // pair_rows == q1)
    pair_turned = dot(order, pair_value)
    lane_r = iota((pairs, full), 1)
    row_r = iota((pairs, full), 0)
    resolved = jnp.broadcast_to(resolved_ref[...].astype(F32), (pairs, full))
    pair_mask = jnp.sum(
        jnp.where(lane_r == group * pair_rows + row_of(row_r), resolved, 0.0),
        axis=1, keepdims=True
    ) * jnp.sum(
        jnp.where(lane_r == rank * aminos + row_r // pair_rows, resolved, 0.0),
        axis=1, keepdims=True)

    for copy in emb_copies:
        copy.wait_recv()
    embedding = emb_buf[...].astype(F32).reshape(rows, ROW_FEATURES)
    normed = layer_normalize(embedding).astype(BF16)
    loads[0].wait()
    projected = dot(normed, proj_ref[...])
    width = HEAD_NUMBER * PER_HEAD_DIM
    queries = (projected[:, :width] * PER_HEAD_DIM ** (-0.5)).astype(BF16)
    keys = projected[:, width:2 * width].astype(BF16)
    values = projected[:, 2 * width:3 * width].astype(BF16)
    gating = jax.nn.sigmoid(projected[:, 3 * width:])

    for copy in aux_copies:
        copy.wait_recv()
    aux = aux_buf[...].astype(F32)
    bias_all = aux[0:ranks, :HEAD_NUMBER]
    for g in range(1, groups):
        bias_all = bias_all + aux[g * ranks:(g + 1) * ranks, :HEAD_NUMBER]
    bias_all = bias_all.reshape(ranks * HEAD_NUMBER, LANES).astype(BF16)
    hq = (HEAD_NUMBER * rows, ranks * HEAD_NUMBER)
    pick = one_hot(
        ((iota(hq, 0) % rows) // tile) * HEAD_NUMBER + iota(hq, 0) // rows == iota(hq, 1))
    bias_q = dot(pick, bias_all)
    hl = (HEAD_NUMBER * rows, LANES)
    bias_q = jnp.where(iota(hl, 1) % aminos == iota(hl, 0) % aminos, bias_q, 0.0).astype(BF16)
    pp = iota((rows, LANES), 0)
    ll = iota((rows, LANES), 1)
    row_pick = one_hot(ll // aminos == (pp // tile) * aminos + pp % aminos)
    bias_full = dot(row_pick, bias_q, 1, 1)
    flag_all = aux[:, HEAD_NUMBER:HEAD_NUMBER + 1].reshape(devices, LANES).astype(BF16)
    near = dot(flag_all, one_hot(pp == rank * tile + ll % tile))
    near_row = jnp.sum(
        jnp.where(
            iota((devices, LANES), 0) == group * ranks + iota((devices, LANES), 1) // tile,
            near, 0.0),
        axis=0, keepdims=True)
    key_mask = (near_row - 1.0) * 1000000000.0
    present = jnp.sum(jnp.where(pp == ll, near_row, 0.0), axis=1, keepdims=True)
    same_chain = (pp // aminos) % per == (ll // aminos) % per
    heads_per = LANES // PER_HEAD_DIM
    mixed = []
    for block in range(width // LANES):
        cols = slice(block * LANES, (block + 1) * LANES)
        total = jnp.zeros((rows, LANES), F32)
        for sub in range(heads_per):
            head = block * heads_per + sub
            lanes = ll // PER_HEAD_DIM == sub
            query = jnp.where(lanes, queries[:, cols], jnp.zeros((), BF16))
            scores = dot(query, keys[:, cols], 1, 1)
            scores = scores + bias_full[:, head * rows:(head + 1) * rows] + key_mask
            scores = jnp.where(same_chain, scores, -3e38)
            exponent = jnp.exp(scores - jnp.max(scores, axis=1, keepdims=True))
            weights = (exponent / jnp.sum(exponent, axis=1, keepdims=True)).astype(BF16)
            total = jnp.where(lanes, dot(weights, values[:, cols]), total)
        mixed.append(total)
    attended = jnp.concatenate(mixed, axis=1).astype(BF16)
    gated = (gating * attended.astype(F32)).astype(BF16)
    loads[1].wait()
    updated = (embedding + dot(gated, final_ref[...])).astype(BF16)
    normed_out = layer_normalize(updated).astype(BF16)

    left_w = jnp.concatenate([lr_ref[:PROJ_FEATURES, :]] * quads, axis=0)
    right_w = jnp.concatenate([lr_ref[PROJ_FEATURES:, :]] * aminos, axis=0)
    left = dot(normed_out, left_w, 1, 1) * present
    left = jnp.where(ll // PROJ_FEATURES == (pp // tile) % quads, left, 0.0)
    for g in range(groups):
        part = left[g * half:g * half + tile]
        for r in range(1, quads):
            part = part + left[g * half + r * tile:g * half + (r + 1) * tile]
        for r in range(ranks):
            side_send[g * ranks + r, :tile] = part.astype(BF16)
    right = dot(normed_out, right_w, 1, 1) * present
    right = jnp.where(ll // PROJ_FEATURES == pp % aminos, right, 0.0).astype(BF16)
    for d in range(devices):
        at = d % ranks * tile
        side_send[d, tile:] = right[at:at + tile]
    out_send[...] = updated.astype(F32).reshape(chains, aminos, ROW_FEATURES).astype(BF16)
    left_copies = []
    for k in range(1, devices):
        peer, device = peer_of(k)
        left_copies.append(send(side_send.at[peer], side_buf.at[me], side_s.at[k], side_r.at[k],
                                device))
    out_copies = []
    for k in range(1, ranks):
        peer = lax.rem(rank + k, ranks)
        out_copies.append(send(out_send.at[pl.ds(peer * per, per)], out_buf.at[own], out_s.at[k], out_r.at[k],
                               {"seq": group, "res": peer}))
    side_buf[me] = side_send[me]
    out_buf[own] = out_send[own]

    gq = (groups * pairs, devices)
    gl = (groups * pairs, LANES)
    within = iota(gl, 0) % pairs
    row_at = group * pair_rows + row_of(within)
    group_q = iota(gq, 0) // pairs
    row_at_q = group * pair_rows + row_of(iota(gq, 0) % pairs)
    row_flags = dot(one_hot(group_q * ranks + row_at_q // aminos == iota(gq, 1)), flag_all)
    col_flags = dot(one_hot(group_q * ranks + rank == iota(gq, 1)), flag_all)
    amino_l = iota(gl, 1) % aminos
    gather_s = one_hot(pp // aminos == ll)
    row_flags = dot(one_hot((amino_l == row_at % aminos) & (row_flags > 0.5)), gather_s)
    col_flags = dot(one_hot((amino_l == within // pair_rows) & (col_flags > 0.5)), gather_s)
    both = jnp.sum(row_flags * col_flags, axis=1, keepdims=True)
    counts = both[:pairs]
    for g in range(1, groups):
        counts = counts + both[g * pairs:(g + 1) * pairs]

    depth = devices * tile
    rep = one_hot(iota((depth, depth), 0) // aminos == iota((depth, depth), 1) // aminos)
    amino_d = iota((depth, LANES), 0) % aminos
    block = iota((pair_rows, LANES), 1) // PROJ_FEATURES
    for copy in left_copies:
        copy.wait_recv()
    left_all = side_buf[:, :tile].reshape(depth, LANES)
    right_all = dot(rep, side_buf[:, tile:].reshape(depth, LANES))
    right_all = jnp.concatenate(
        [jnp.where(amino_d == a, right_all, 0.0).astype(BF16) for a in range(aminos)], axis=1)
    product = dot(left_all, right_all, 0, 0)
    for a in range(aminos):
        product_buf[a * LANES:(a + 1) * LANES, :] = product[:, a * LANES:(a + 1) * LANES]
    for c in range(0, PROJ_FEATURES, aminos):
        slabs = [product_buf[pl.ds(c + x, pair_rows, stride=PROJ_FEATURES), :]
                 for x in range(aminos)]
        for j in range(aminos):
            turned = jnp.zeros((pair_rows, LANES), F32)
            for x in range(aminos):
                shift = (x - j) % aminos * PROJ_FEATURES
                moved = pltpu.roll(slabs[x], shift, 1) if shift else slabs[x]
                turned = jnp.where(block == x, moved, turned)
            lhs_buf[j * pair_rows:(j + 1) * pair_rows,
                    c * PROJ_FEATURES:c * PROJ_FEATURES + LANES] = turned.astype(BF16)
    loads[2].wait()
    outer = dot(lhs_buf[...], outer_ref[...])
    result = (pair_turned + pair_mask * (outer / counts)).astype(BF16)
    pair_out_ref[...] = dot(order, result, 0, 0).astype(BF16)

    for copy in out_copies:
        copy.wait_recv()
    out_ref[...] = out_buf[...]
    for copy in emb_copies + aux_copies + left_copies + out_copies:
        copy.wait_send()


def fused(*args):
    emb, mask, resolved, pair = args[:4]
    groups, ranks = lax.axis_size("seq"), lax.axis_size("res")
    chains, aminos = emb.shape[:2]
    tile = chains // ranks * aminos
    pair_rows = pair.shape[0]
    devices = groups * ranks
    vmem = pl.BlockSpec(memory_space=pltpu.VMEM)
    whole = pl.BlockSpec(memory_space=pl.ANY)
    dma = pltpu.SemaphoreType.DMA
    out, pair_out = pl.pallas_call(
        functools.partial(fused_kernel, groups, ranks, chains, aminos),
        out_shape=(
            jax.ShapeDtypeStruct(emb.shape, BF16),
            jax.ShapeDtypeStruct((pair_rows * aminos, CZ), BF16),
        ),
        in_specs=[vmem] * 4 + [whole, vmem, whole, vmem, whole],
        out_specs=(vmem, vmem),
        scratch_shapes=[
            pltpu.VMEM(emb.shape, BF16),
            pltpu.VMEM((devices, 2 * HEAD_NUMBER, LANES), BF16),
            pltpu.VMEM((devices, 2 * tile, LANES), BF16),
            pltpu.VMEM((devices, 2 * tile, LANES), BF16),
            pltpu.VMEM(emb.shape, BF16),
            pltpu.VMEM(emb.shape, BF16),
            pltpu.VMEM((pair_rows * PROJ_FEATURES, LANES), F32),
            pltpu.VMEM((pair_rows * aminos, PROJ_FEATURES * PROJ_FEATURES), BF16),
            pltpu.VMEM(args[4].shape, BF16),
            pltpu.VMEM(args[6].shape, BF16),
            pltpu.VMEM(args[8].shape, BF16),
            dma((ranks,)), dma((ranks,)), dma((devices,)), dma((devices,)),
            dma((devices,)), dma((devices,)), dma((ranks,)), dma((ranks,)), dma((3,)),
        ],
        compiler_params=pltpu.CompilerParams(collective_id=0, has_side_effects=True),
    )(
        emb, mask.T, resolved.reshape(1, -1),
        pair.reshape(-1, CZ), args[4], args[5].T, args[6], args[7].T, args[8],
    )
    return out, pair_out.reshape(pair.shape)


def fits(mesh, emb, pair):
    groups, ranks = mesh.shape["seq"], mesh.shape["res"]
    chains, aminos = emb.shape[:2]
    if chains % ranks or aminos * PROJ_FEATURES != LANES or chains * aminos != LANES:
        return False
    pairs = pair.shape[0] * aminos
    return pairs * groups == LANES and chains // ranks * aminos * groups == PROJ_FEATURES


def solution(mesh):
    placed = (
        P(("crop", "seq"), "res", None),
        P(("crop", "seq"), "res"),
        P("crop"),
        P(("crop", "seq"), "res", None),
        P(),
        P(),
        P(),
        P(),
        P(),
    )
    def either(*args):
        return (fused if fits(mesh, args[0], args[3]) else per_device)(*args)

    return jax.shard_map(
        either,
        mesh=mesh,
        in_specs=placed,
        out_specs=(P(("crop", "seq"), "res", None), P(("crop", "seq"), "res", None)),
        check_vma=False,
    )
```

profile of v0, /device:TPU:0, one launch (start us, length us, event | category | flops | bytes accessed | tf_op | source)
XLA Modules:
  0.0 25.3 jit_solution(11983556159739749718)
XLA Ops:
  0.6 22.6 %shard_map.104 = (bf16[32,4,256]{2,1,0:T(4,128)(2,1)}, bf16[64,128]{1,0:T(8,128)(2,1)}) custom-call(bf16[32,4,256]{2,1,0:T(4,128)(2,1)} %emb_ref.1, s32[4,32]{1,0:T(4,128)} %bitcast.9, s32[1,32]{1,0:T(1,128)} %bitcast.11, bf16[64,128]{1,0:T(8,128)(2,1)} %bitcast.7, bf16[256,1024]{1,0:T(8,128)(2,1)} %proj_hbm.1, bf16[8,128]{1,0:T(8,128)(2,1)} %bitcast.10, ...), custom_call_target="tpu_custom_call" | custom-call | tf_op jit(solution)/shard_map/pallas_call | solution.py:442
  23.2 0.0 copy-start
  23.2 1.5 %copy.13 = bf16[32,4,256]{2,1,0:T(4,128)(2,1)} copy(bf16[32,4,256]{2,1,0:T(4,128)(2,1)} %get-tuple-element.8) | data formatting | bytes 131072
  24.7 0.0 copy-done
  24.7 0.6 %copy.14 = bf16[16,4,128]{2,1,0:T(4,128)(2,1)} copy(bf16[16,4,128]{2,1,0:T(4,128)(2,1)S(1)} %bitcast.8) | data formatting | bytes 32768
Async XLA Ops:
  23.2 1.5 %copy-start = (bf16[64,128]{1,0:T(8,128)(2,1)S(1)}, bf16[64,128]{1,0:T(8,128)(2,1)}, u32[]{:S(2)}) copy-start(bf16[64,128]{1,0:T(8,128)(2,1)} %get-tuple-element.5) | copy-start | bytes 49156
where the time goes:
time: 25.7 us; the launch traced here: 25.3 us
  Pallas kernels  22.6 us (88%)
  local copies, waits for them, and re-layouts  2.11 us (8%)
  between operations  0.65 us (3%)
    pallas_call x1, Pallas kernels, fused(): pl.pallas_call(functools.partial(fused_kernel, groups, ranks, chains, ami...  22.6 us
    unnamed x4, local copies, waits for them, and re-layouts  2.11 us

commit v1 on v0

v1 whole, which is shorter than its diff:
```python
import functools
import math

import jax
import jax.numpy as jnp
from jax import lax
from jax.experimental import pallas as pl
from jax.experimental.pallas import tpu as pltpu
from jax.sharding import PartitionSpec as P

ROW_FEATURES = 256
CZ = 128
HEAD_NUMBER = 8
PER_HEAD_DIM = 32
PROJ_FEATURES = 32


epsilon = 1e-05


def layer_normalize(values):
    values = values.astype(jnp.float32)
    average = jnp.mean(values, axis=-1, keepdims=True)
    centered = values - average
    variance = jnp.mean(centered * centered, axis=-1, keepdims=True)
    return centered * lax.rsqrt(variance + epsilon)


def outer_rows(left_side, right_side, project):
    row_total = left_side.shape[1]
    col_total = right_side.shape[1]
    block_rows = math.gcd(row_total, max(1, 2048 // col_total))

    def outer_block(start):
        product = jnp.einsum(
            "sic,sje->ijce", left_side, right_side, preferred_element_type=jnp.float32
        )
        flattened = product.reshape(block_rows * col_total, PROJ_FEATURES * PROJ_FEATURES)
        return jnp.dot(flattened, project, precision=lax.Precision.HIGHEST).reshape(
            block_rows, col_total, CZ
        )

    starts = jnp.arange(row_total // block_rows, dtype=jnp.int32) * block_rows
    return lax.map(outer_block, starts).reshape(row_total, col_total, CZ)


def per_device(
    aligned_chain_embedding,
    alignment_mask,
    resolved_residue_mask,
    pairwise_state,
    combined_projection_matrix,
    pair_bias_weight,
    final_projection_matrix,
    left_right_projection_matrix,
    outer_mean_weight,
):
    chain_count = aligned_chain_embedding.shape[0]
    amino_count = aligned_chain_embedding.shape[1]
    res_ranks = lax.axis_size("res")
    seq_groups = lax.axis_size("seq")
    full_length = amino_count * res_ranks
    row_count = full_length // seq_groups
    item_count = HEAD_NUMBER * chain_count // res_ranks
    per_head = min(item_count, chain_count)
    head_count = item_count // per_head
    my_rank = lax.axis_index("res")
    my_group = lax.axis_index("seq")
    standardized_rows = layer_normalize(aligned_chain_embedding).astype(jnp.bfloat16)
    linear_mapped = jnp.dot(
        standardized_rows.reshape(chain_count * amino_count, ROW_FEATURES),
        combined_projection_matrix,
        preferred_element_type=jnp.float32,
    )
    linear_mapped = linear_mapped.reshape(chain_count, amino_count, 4, HEAD_NUMBER, PER_HEAD_DIM)
    queries = (linear_mapped[:, :, 0] * PER_HEAD_DIM ** (-0.5)).astype(jnp.bfloat16)
    key_rows = linear_mapped[:, :, 1].astype(jnp.bfloat16)
    value_rows = linear_mapped[:, :, 2].astype(jnp.bfloat16)
    sigmoid_factor = jax.nn.sigmoid(linear_mapped[:, :, 3])
    stacked = jnp.stack([queries, key_rows, value_rows], axis=2)
    stacked = jnp.transpose(stacked, (3, 0, 1, 2, 4)).reshape(
        HEAD_NUMBER * chain_count, amino_count, 3 * PER_HEAD_DIM
    )
    presence_mask_flags = alignment_mask.astype(jnp.bfloat16)
    key_flags = jnp.broadcast_to(
        presence_mask_flags[None], (HEAD_NUMBER, chain_count, amino_count)
    ).reshape(HEAD_NUMBER * chain_count, amino_count)
    arrived, arrived_flags = (
        lax.all_to_all(stacked, "res", split_axis=0, concat_axis=1, tiled=True),
        lax.all_to_all(key_flags, "res", split_axis=0, concat_axis=1, tiled=True),
    )
    pair_normed = layer_normalize(pairwise_state).astype(jnp.bfloat16)
    local_bias = jnp.dot(
        pair_normed.reshape(row_count * amino_count, CZ),
        pair_bias_weight,
        preferred_element_type=jnp.float32,
    )
    local_bias = jnp.transpose(
        local_bias.astype(jnp.bfloat16).reshape(row_count, amino_count, HEAD_NUMBER), (2, 0, 1)
    )
    bias_cols = lax.all_gather(local_bias, "res", axis=2, tiled=True)
    whole_bias = lax.all_gather(bias_cols, "seq", axis=1, tiled=True)
    first_head = my_rank * item_count // chain_count
    head_bias = lax.dynamic_slice_in_dim(whole_bias, first_head, head_count, 0)
    grouped = arrived.reshape(head_count, per_head, full_length, 3, PER_HEAD_DIM)
    key_validity_mask = (
        arrived_flags.reshape(head_count, per_head, full_length).astype(jnp.float32) - 1.0
    ) * 1000000000.0
    scores = jnp.einsum(
        "gpid,gpjd->gpij",
        grouped[:, :, :, 0],
        grouped[:, :, :, 1],
        preferred_element_type=jnp.float32,
    )
    scores = scores + head_bias.astype(jnp.float32)[:, None] + key_validity_mask[:, :, None, :]
    row_max = jnp.max(scores, axis=-1, keepdims=True)
    exponent = jnp.exp(scores - row_max)
    weights = (exponent / jnp.sum(exponent, axis=-1, keepdims=True)).astype(jnp.bfloat16)
    softmax_mixed = jnp.einsum(
        "gpij,gpjd->gpid", weights, grouped[:, :, :, 2], preferred_element_type=jnp.float32
    )
    softmax_mixed = softmax_mixed.astype(jnp.bfloat16).reshape(
        item_count, full_length, PER_HEAD_DIM
    )
    returned = lax.all_to_all(softmax_mixed, "res", split_axis=1, concat_axis=0, tiled=True)
    returned = jnp.transpose(
        returned.reshape(HEAD_NUMBER, chain_count, amino_count, PER_HEAD_DIM), (1, 2, 0, 3)
    )
    sigmoid_scaled = (
        (sigmoid_factor * returned.astype(jnp.float32))
        .astype(jnp.bfloat16)
        .reshape(chain_count * amino_count, ROW_FEATURES)
    )
    embedding_increment = jnp.dot(
        sigmoid_scaled, final_projection_matrix, preferred_element_type=jnp.float32
    ).reshape(chain_count, amino_count, ROW_FEATURES)
    alignment_output = (aligned_chain_embedding.astype(jnp.float32) + embedding_increment).astype(
        jnp.bfloat16
    )
    standardized_product = layer_normalize(alignment_output).astype(jnp.bfloat16)
    left_right_vectors = jnp.dot(
        standardized_product.reshape(chain_count * amino_count, ROW_FEATURES),
        left_right_projection_matrix,
        preferred_element_type=jnp.float32,
    )
    left_right_vectors = left_right_vectors.reshape(chain_count, amino_count, 2, PROJ_FEATURES)
    entry_present = alignment_mask.astype(jnp.float32)[:, :, None]
    left_side = (left_right_vectors[:, :, 0] * entry_present).astype(jnp.bfloat16)
    right_side = (left_right_vectors[:, :, 1] * entry_present).astype(jnp.bfloat16)
    left_all, left_flags = (
        lax.all_gather(left_side, "res", axis=1, tiled=True),
        lax.all_gather(presence_mask_flags, "res", axis=1, tiled=True),
    )
    project = outer_mean_weight.astype(jnp.float32)
    row_start = my_group * row_count
    left_full, flag_full = (
        lax.all_to_all(left_all, "seq", split_axis=1, concat_axis=0, tiled=True),
        lax.all_to_all(left_flags, "seq", split_axis=1, concat_axis=0, tiled=True),
    )
    right_full, right_flags = (
        lax.all_gather(right_side, "seq", axis=0, tiled=True),
        lax.all_gather(presence_mask_flags, "seq", axis=0, tiled=True),
    )
    counts = jnp.dot(flag_full.T, right_flags, preferred_element_type=jnp.float32)
    outer = outer_rows(left_full, right_full, project)
    col_start = my_rank * amino_count
    row_mask = lax.dynamic_slice_in_dim(resolved_residue_mask, row_start, row_count).astype(
        jnp.float32
    )
    col_mask = lax.dynamic_slice_in_dim(resolved_residue_mask, col_start, amino_count).astype(
        jnp.float32
    )
    pair_mask = row_mask[:, None] * col_mask[None, :]
    pairwise_output = (
        pairwise_state.astype(jnp.float32) + pair_mask[:, :, None] * (outer / counts[:, :, None])
    ).astype(jnp.bfloat16)
    return (alignment_output, pairwise_output)


LANES = 128
F32 = jnp.float32
BF16 = jnp.bfloat16


def iota(shape, axis):
    return lax.broadcasted_iota(jnp.int32, shape, axis)


def dot(a, b, ca=1, cb=0):
    return lax.dot_general(a, b, (((ca,), (cb,)), ((), ())), preferred_element_type=F32)


def one_hot(cond):
    return jnp.where(cond, 1.0, 0.0).astype(BF16)


def flat(block):
    return block.reshape(-1, block.shape[-1])


def fused_kernel(
    groups, ranks, per, aminos,
    emb_hbm, mask_hbm, resolved_hbm, pair_hbm, proj_hbm, bias_hbm, final_hbm, lr_hbm, outer_hbm,
    out_ref, pair_out_ref,
    emb_in, mask_ref, resolved_ref, pair_ref, proj_ref, bias_w_ref, final_ref, lr_ref, outer_ref,
    emb_buf, flag_buf, bias_buf, left_send, right_send, left_buf, right_buf, out_send,
    product_buf, lhs_buf, turn_buf,
    load_s, emb_s, emb_r, out_s, out_r,
    flag_s, flag_r, bias_s, bias_r, left_s, left_r, right_s, right_r,
):
    devices = groups * ranks
    chains = per * ranks
    full = ranks * aminos
    rows = per * full
    pair_rows = full // groups
    pairs = pair_rows * aminos
    quads = pair_rows // aminos
    width = HEAD_NUMBER * PER_HEAD_DIM
    halves = width // LANES
    heads_per = LANES // PER_HEAD_DIM
    slot = LANES // groups
    group = lax.axis_index("seq")
    rank = lax.axis_index("res")
    me = group * ranks + rank

    def flip(k):
        peer = 0
        for bit in range(ranks.bit_length() - 1):
            digit = rank // (1 << bit) % 2
            peer = peer + (1 << bit) * (1 - digit if k >> bit & 1 else digit)
        return peer

    others = []
    for shift in range(groups - 1, -1, -1):
        for k in range(ranks - 1, -1, -1):
            if shift or k:
                others.append((shift * ranks + k, lax.rem(group + shift, groups), flip(k)))

    def where_is(g, r):
        return {"seq": g, "res": r}

    barrier = pltpu.get_barrier_semaphore()
    for _, g, r in others:
        pl.semaphore_signal(
            barrier, inc=1, device_id=where_is(g, r), device_id_type=pl.DeviceIdType.MESH
        )

    def load(k, src, dst):
        copy = pltpu.make_async_copy(src, dst, load_s.at[k])
        copy.start()
        return copy

    pair_load = load(0, pair_hbm, pair_ref)
    bias_load = load(1, bias_hbm, bias_w_ref)
    mask_load = load(2, mask_hbm, mask_ref)
    emb_load = load(3, emb_hbm, emb_in)
    proj_load = load(4, proj_hbm, proj_ref)
    final_load = load(5, final_hbm, final_ref)
    lr_load = load(6, lr_hbm, lr_ref)
    outer_load = load(7, outer_hbm, outer_ref)
    resolved_load = load(8, resolved_hbm, resolved_ref)

    def send(src, dst, ssem, rsem, device):
        copy = pltpu.make_async_remote_copy(
            src_ref=src, dst_ref=dst, send_sem=ssem, recv_sem=rsem,
            device_id=device, device_id_type=pl.DeviceIdType.MESH,
        )
        copy.start()
        return copy

    def take(view, sem):
        pltpu.make_async_copy(view, view, sem).wait()

    rest, near_rest = pl.ds(0, devices - 1), pl.ds(0, per * (ranks - 1))
    bias_all, flag_all, right_all = bias_buf.at[rest], flag_buf.at[rest], right_buf.at[rest]
    left_all = left_buf.at[:, rest]
    emb_all, out_all = emb_in.at[near_rest], out_ref.at[near_rest]

    bias_load.wait()
    lane_head = iota((LANES, HEAD_NUMBER), 0)
    lane_head = (lane_head // slot + group) % groups * heads_per + lane_head % slot // pair_rows
    wide_w = dot(one_hot(lane_head == iota((LANES, HEAD_NUMBER), 1)), bias_w_ref[...]).astype(BF16)
    mask_load.wait()
    flags = dot(mask_ref[...].astype(F32).astype(BF16), one_hot(
        iota((chains, LANES), 0) == iota((chains, LANES), 1)))
    flag_buf[me] = flags.astype(BF16)
    pair_load.wait()
    pair_value = flat(pair_ref[...].astype(F32))
    own_bias = dot(layer_normalize(pair_value).astype(BF16), wide_w, 1, 1)
    own_bias = jnp.where(
        iota((pairs, LANES), 0) // aminos == iota((pairs, LANES), 1) % pair_rows, own_bias, 0.0)
    own_bias = jnp.sum(own_bias.reshape(pair_rows, aminos, LANES), axis=0)
    bias_buf[me] = own_bias.astype(BF16)
    own = pl.ds(rank * per, per)
    emb_load.wait()
    emb_buf[:, pl.ds(rank, 1)] = emb_in[own][:, None]

    pl.semaphore_wait(barrier, devices - 1)
    for k, g, r in others:
        send(bias_buf.at[me], bias_buf.at[me], bias_s, bias_r,
                                where_is(g, r))
    for k, g, r in others:
        if k < ranks:
            send(emb_in.at[pl.ds(r * per, per)], emb_buf.at[:, rank],
                                   emb_s, emb_r, where_is(g, r))
    for k, g, r in others[::-1]:
        send(flag_buf.at[me], flag_buf.at[me], flag_s, flag_r,
                                where_is(g, r))

    heads_q = heads_per * pair_rows
    block_mask = (iota((LANES, LANES), 0) % slot // pair_rows
                  == iota((LANES, LANES), 1) // PER_HEAD_DIM)
    take(emb_all, emb_r)
    embedding = emb_buf[...].astype(F32).reshape(rows, ROW_FEATURES)
    normed = layer_normalize(embedding).astype(BF16)
    proj_load.wait()
    projected = dot(normed, proj_ref[...])
    queries = (projected[:, :width] * PER_HEAD_DIM ** (-0.5)).astype(BF16)
    keys = projected[:, width:2 * width].astype(BF16)
    values = projected[:, 2 * width:3 * width].astype(BF16)
    gating = jax.nn.sigmoid(projected[:, 3 * width:])

    raw = {}
    for b in range(halves):
        cols = slice(b * LANES, (b + 1) * LANES)
        for c in range(per):
            spread = []
            for s in range(groups):
                at = c * full + (b - s) % groups * pair_rows
                spread += [queries[at:at + pair_rows, cols]] * heads_per
            spread = jnp.concatenate(spread, axis=0)
            spread = jnp.where(block_mask, spread, jnp.zeros_like(spread))
            raw[b, c] = dot(keys[c * full:(c + 1) * full, cols], spread, 1, 1)

    take(flag_all, flag_r)
    near = flat(flag_buf[pl.ds(group * ranks, ranks)])
    pick = one_hot(iota((LANES, per * LANES), 0)
                   == rank * per + iota((LANES, per * LANES), 1) // LANES)
    key_flags = dot(near, pick)
    key_mask = (key_flags - 1.0) * 1000000000.0
    present = jnp.concatenate(
        [key_flags[:, c * LANES:(c + 1) * LANES] for c in range(per)], axis=0)

    take(bias_all, bias_r)
    bias = [flat(bias_buf[pl.ds(g * ranks, ranks)]).astype(F32) for g in range(groups)]
    which = iota((full, LANES), 1) // slot
    mixed = []
    for b in range(halves):
        cols = slice(b * LANES, (b + 1) * LANES)
        tile_bias = bias[b % groups]
        for s in range(1, groups):
            tile_bias = jnp.where(which == s, bias[(b - s) % groups], tile_bias)
        weights, blocks = [], []
        for c in range(per):
            scores = raw[b, c] + tile_bias + key_mask[:, c * LANES:(c + 1) * LANES]
            exponent = jnp.exp(scores - jnp.max(scores, axis=0, keepdims=True))
            total = 1.0 / jnp.sum(exponent, axis=0, keepdims=True)
            weights.append((exponent * total).astype(BF16))
            own_values = values[c * full:(c + 1) * full, cols]
            blocks.append(jnp.concatenate(
                [own_values if d == c else jnp.zeros_like(own_values) for d in range(per)], axis=1))
        weights = jnp.concatenate(weights, axis=0)
        blocks = jnp.concatenate(blocks, axis=0)
        summed = dot(weights, blocks, 0, 0)
        lane_h = iota((pair_rows, LANES), 1) // PER_HEAD_DIM
        parts = []
        for c in range(per):
            for g in range(groups):
                at = (b - g) % groups * slot
                part = summed[at:at + pair_rows, c * LANES:(c + 1) * LANES]
                for h in range(1, heads_per):
                    row = at + h * pair_rows
                    part = jnp.where(
                        lane_h == h,
                        summed[row:row + pair_rows, c * LANES:(c + 1) * LANES], part)
                parts.append(part)
        mixed.append(jnp.concatenate(parts, axis=0))
    attended = jnp.concatenate(mixed, axis=1).astype(BF16)
    gated = (gating * attended.astype(F32)).astype(BF16)
    final_load.wait()
    lr_load.wait()
    updated = (embedding + dot(gated, final_ref[...])).astype(BF16)
    normed_out = layer_normalize(updated).astype(BF16)
    sides_w = jnp.concatenate(
        [lr_ref[:PROJ_FEATURES, :]] * aminos + [lr_ref[PROJ_FEATURES:, :]] * aminos, axis=0)
    sides = dot(normed_out, sides_w, 1, 1)
    two = (rows, 2 * LANES)
    sides = (sides * jnp.concatenate([present] * 2, axis=1)).astype(BF16)
    sides = jnp.where(iota(two, 1) // PROJ_FEATURES % aminos == iota(two, 0) % aminos,
                      sides, jnp.zeros_like(sides))
    sq = (chains, rows)
    gather = one_hot((iota(sq, 0) // per == iota(sq, 1) % full // aminos)
                     & (iota(sq, 0) % per == iota(sq, 1) // full))
    sides = dot(gather, sides).reshape(ranks, per, 2 * LANES).astype(BF16)
    left_send[...] = sides[:, :, :LANES]
    right_send[...] = sides[:, :, LANES:]
    for k, g, r in others:
        send(left_send.at[pl.ds(g * quads, quads)], left_buf.at[:, me],
                                left_s, left_r, where_is(g, r))
        send(right_send.at[r], right_buf.at[me],
                                 right_s, right_r, where_is(g, r))
    out_send[...] = updated.astype(F32).reshape(per, ranks, aminos, ROW_FEATURES).astype(BF16)
    for k, g, r in others:
        if k < ranks:
            send(out_send.at[:, r], out_ref.at[own],
                                   out_s, out_r, where_is(g, r))
    left_buf[:, pl.ds(me, 1)] = left_send[pl.ds(group * quads, quads)][:, None]
    right_buf[me] = right_send[rank]
    out_ref[own] = out_send[:, pl.ds(rank, 1)].reshape(per, aminos, ROW_FEATURES)

    at = (pairs, full)
    row_pick = iota(at, 1) == group * pair_rows + iota(at, 0) // aminos
    col_pick = iota(at, 1) == rank * aminos + iota(at, 0) % aminos
    both = jnp.zeros((pairs, LANES), F32)
    for g in range(groups):
        seen = flat(flag_buf[pl.ds(g * ranks, ranks)])
        both = both + dot(one_hot(row_pick), seen) * dot(one_hot(col_pick), seen)
    counts = jnp.sum(both, axis=1, keepdims=True)
    resolved_load.wait()
    resolved = jnp.broadcast_to(resolved_ref[...].astype(F32), at)
    scale = jnp.sum(jnp.where(row_pick, resolved, 0.0), axis=1, keepdims=True) * jnp.sum(
        jnp.where(col_pick, resolved, 0.0), axis=1, keepdims=True) / counts
    scale = jnp.broadcast_to(scale, (pairs, LANES))
    outer_load.wait()
    block = iota((pair_rows, LANES), 1) // PROJ_FEATURES
    take(right_all, right_r)
    take(left_all, left_r)
    right_rows = flat(right_buf[...])
    for q in range(quads):
        product_buf[q * LANES:(q + 1) * LANES, :] = dot(flat(left_buf[q]), right_rows, 0, 0)
    for c in range(0, PROJ_FEATURES, aminos):
        slabs = [product_buf[pl.ds(c + x, pair_rows, stride=PROJ_FEATURES), :]
                 for x in range(aminos)]
        for j in range(aminos):
            turned = jnp.zeros((pair_rows, LANES), F32)
            for x in range(aminos):
                shift = (x - j) % aminos * PROJ_FEATURES
                moved = pltpu.roll(slabs[x], shift, 1) if shift else slabs[x]
                turned = jnp.where(block == x, moved, turned)
            lhs_buf[j * pair_rows:(j + 1) * pair_rows,
                    c * PROJ_FEATURES:c * PROJ_FEATURES + LANES] = turned.astype(BF16)
    outer = dot(lhs_buf[...], outer_ref[...])
    for j in range(aminos):
        turn_buf[pl.ds(j, pair_rows, stride=aminos), :] = outer[j * pair_rows:(j + 1) * pair_rows]
    result = pair_value + scale * turn_buf[...]
    pair_out_ref[...] = result.reshape(pair_rows, aminos, CZ).astype(BF16)
    take(out_all, out_r)
    for view, sem in ((bias_all, bias_s), (emb_all, emb_s), (flag_all, flag_s),
                      (left_all, left_s), (right_all, right_s), (out_all, out_s)):
        take(view, sem)


def write_kernel(out_ref, pair_ref, out_hbm, pair_hbm, sem):
    copies = [pltpu.make_async_copy(out_ref, out_hbm, sem.at[0]),
              pltpu.make_async_copy(pair_ref, pair_hbm, sem.at[1])]
    for copy in copies:
        copy.start()
    for copy in copies:
        copy.wait()


def fused(*args):
    emb, mask, resolved, pair = args[:4]
    groups, ranks = lax.axis_size("seq"), lax.axis_size("res")
    chains, aminos = emb.shape[:2]
    per = chains // ranks
    pair_rows = pair.shape[0]
    quads = pair_rows // aminos
    devices = groups * ranks
    operands = (emb, mask.T, resolved.reshape(1, -1), pair, args[4], args[5].T, args[6],
                args[7].T, args[8])
    vmem = pl.BlockSpec(memory_space=pltpu.VMEM)
    whole = pl.BlockSpec(memory_space=pl.ANY)
    dma = pltpu.SemaphoreType.DMA
    results = pl.pallas_call(
        functools.partial(fused_kernel, groups, ranks, per, aminos),
        out_shape=(pltpu.VMEM(emb.shape, BF16), pltpu.VMEM(pair.shape, BF16)),
        in_specs=[whole] * len(operands),
        out_specs=(vmem, vmem),
        scratch_shapes=[pltpu.VMEM(x.shape, x.dtype) for x in operands] + [
            pltpu.VMEM((per, ranks, aminos, ROW_FEATURES), BF16),
            pltpu.VMEM((devices, aminos, LANES), BF16),
            pltpu.VMEM((devices, aminos, LANES), BF16),
            pltpu.VMEM((ranks, per, LANES), BF16),
            pltpu.VMEM((ranks, per, LANES), BF16),
            pltpu.VMEM((quads, devices, per, LANES), BF16),
            pltpu.VMEM((devices, per, LANES), BF16),
            pltpu.VMEM((per, ranks, aminos, ROW_FEATURES), BF16),
            pltpu.VMEM((pair_rows * PROJ_FEATURES, LANES), F32),
            pltpu.VMEM((pair_rows * aminos, PROJ_FEATURES * PROJ_FEATURES), BF16),
            pltpu.VMEM((pair_rows * aminos, CZ), F32),
            dma((len(operands),)),
        ] + [dma] * 12,
        compiler_params=pltpu.CompilerParams(collective_id=0, has_side_effects=True),
    )(*operands)
    return pl.pallas_call(
        write_kernel,
        out_shape=(jax.ShapeDtypeStruct(emb.shape, BF16), jax.ShapeDtypeStruct(pair.shape, BF16)),
        in_specs=[whole, whole],
        out_specs=(whole, whole),
        scratch_shapes=[dma((2,))],
    )(*[pltpu.with_memory_space_constraint(x, pltpu.VMEM) for x in results])


def fits(mesh, emb, pair):
    groups, ranks = mesh.shape["seq"], mesh.shape["res"]
    chains, aminos = emb.shape[:2]
    if chains % ranks or aminos * PROJ_FEATURES != LANES or chains * aminos != LANES:
        return False
    if ranks & (ranks - 1) or HEAD_NUMBER * PER_HEAD_DIM != groups * LANES:
        return False
    pairs = pair.shape[0] * aminos
    return pairs * groups == LANES and chains // ranks * aminos * groups == PROJ_FEATURES


def solution(mesh):
    placed = (
        P(("crop", "seq"), "res", None),
        P(("crop", "seq"), "res"),
        P("crop"),
        P(("crop", "seq"), "res", None),
        P(),
        P(),
        P(),
        P(),
        P(),
    )
    def either(*args):
        return (fused if fits(mesh, args[0], args[3]) else per_device)(*args)

    return jax.shard_map(
        either,
        mesh=mesh,
        in_specs=placed,
        out_specs=(P(("crop", "seq"), "res", None), P(("crop", "seq"), "res", None)),
        check_vma=False,
    )
```

time: 25.7 us -> 18.9 us (0.74)
  Pallas kernels: 22.6 us -> 18.1 us
  local copies, waits for them, and re-layouts: 2.11 us -> 0 us
    pallas_call x1 -> x2, Pallas kernels: 22.6 us -> 18.1 us  [the longest x1 17.5 us: fused(): pl.pallas_call(functools.partial(fused_kernel, groups, ranks, per, aminos...]
    unnamed x4 -> x0, local copies, waits for them, and re-layouts: 2.11 us -> none
where the time goes in v1:
time: 18.9 us; the launch traced here: 18.8 us
  Pallas kernels  18.1 us (96%)
  between operations  0.64 us (3%)
    pallas_call x1, Pallas kernels, fused(): pl.pallas_call(functools.partial(fused_kernel, groups, ranks, per, aminos...  17.5 us
    pallas_call x1, Pallas kernels, fused(): pl.pallas_call(write_kernel, out_shape=(jax.ShapeDtypeStruct(emb.shape, B...  0.65 us

profile of v1, /device:TPU:0, one launch (start us, length us, event | category | flops | bytes accessed | tf_op | source)
XLA Modules:
  0.0 18.8 jit_solution(6597961509709488316)
XLA Ops:
  0.6 17.5 %shard_map.104 = (bf16[32,4,256]{2,1,0:T(4,128)(2,1)S(1)}, bf16[16,4,128]{2,1,0:T(4,128)(2,1)S(1)}) custom-call(bf16[32,4,256]{2,1,0:T(4,128)(2,1)} %emb_hbm.1, s32[4,32]{1,0:T(4,128)} %bitcast.5, s32[1,32]{1,0:T(1,128)} %bitcast.7, bf16[16,4,128]{2,1,0:T(4,128)(2,1)} %pair_hbm.1, bf16[256,1024]{1,0:T(8,128)(2,1)} %proj_hbm.1, bf16[8,128]{1,0:T(8,128)(2,1)} %bitcast.6, ...), custom_call_target="tpu_custom_call" | custom-call | tf_op jit(solution)/shard_map/pallas_call | solution.py:475
  18.1 0.7 %shard_map.105 = (bf16[32,4,256]{2,1,0:T(4,128)(2,1)}, bf16[16,4,128]{2,1,0:T(4,128)(2,1)}) custom-call(bf16[32,4,256]{2,1,0:T(4,128)(2,1)S(1)} %get-tuple-element.4.out_ref, bf16[16,4,128]{2,1,0:T(4,128)(2,1)S(1)} %get-tuple-element.5.pair_ref), custom_call_target="tpu_custom_call" | custom-call | tf_op jit(solution)/shard_map/pallas_call | solution.py:496

commit v2 on v1

--- a/solution.py
+++ b/solution.py
@@ -202,11 +202,9 @@
     groups, ranks, per, aminos,
     emb_hbm, mask_hbm, resolved_hbm, pair_hbm, proj_hbm, bias_hbm, final_hbm, lr_hbm, outer_hbm,
     out_ref, pair_out_ref,
-    emb_in, mask_ref, resolved_ref, pair_ref, proj_ref, bias_w_ref, final_ref, lr_ref, outer_ref,
-    emb_buf, flag_buf, bias_buf, left_send, right_send, left_buf, right_buf, out_send,
-    product_buf, lhs_buf, turn_buf,
-    load_s, emb_s, emb_r, out_s, out_r,
-    flag_s, flag_r, bias_s, bias_r, left_s, left_r, right_s, right_r,
+    pack, near, far, mask_ref, resolved_ref, pair_ref, proj_ref, bias_w_ref, final_ref, lr_ref,
+    outer_ref, side_send, side_buf, out_send, raw_buf, mask_buf, gate_buf, value_buf,
+    product_buf, turn_buf, load_s, send_s, near_r, far_r, side_r, out_r,
 ):
     devices = groups * ranks
     chains = per * ranks
@@ -236,13 +234,10 @@
             if shift or k:
                 others.append((shift * ranks + k, lax.rem(group + shift, groups), flip(k)))
 
-    def where_is(g, r):
-        return {"seq": g, "res": r}
-
     barrier = pltpu.get_barrier_semaphore()
     for _, g, r in others:
         pl.semaphore_signal(
-            barrier, inc=1, device_id=where_is(g, r), device_id_type=pl.DeviceIdType.MESH
+            barrier, inc=1, device_id={"seq": g, "res": r}, device_id_type=pl.DeviceIdType.MESH
         )
 
     def load(k, src, dst):
@@ -250,31 +245,30 @@
         copy.start()
         return copy
 
-    pair_load = load(0, pair_hbm, pair_ref)
-    bias_load = load(1, bias_hbm, bias_w_ref)
-    mask_load = load(2, mask_hbm, mask_ref)
-    emb_load = load(3, emb_hbm, emb_in)
+    emb_load = load(0, emb_hbm, pack.at[:, pl.ds(0, per)])
+    pair_load = load(1, pair_hbm, pair_ref)
+    bias_load = load(2, bias_hbm, bias_w_ref)
+    mask_load = load(3, mask_hbm, mask_ref)
     proj_load = load(4, proj_hbm, proj_ref)
     final_load = load(5, final_hbm, final_ref)
     lr_load = load(6, lr_hbm, lr_ref)
-    outer_load = load(7, outer_hbm, outer_ref)
-    resolved_load = load(8, resolved_hbm, resolved_ref)
-
-    def send(src, dst, ssem, rsem, device):
-        copy = pltpu.make_async_remote_copy(
-            src_ref=src, dst_ref=dst, send_sem=ssem, recv_sem=rsem,
-            device_id=device, device_id_type=pl.DeviceIdType.MESH,
-        )
-        copy.start()
-        return copy
+    resolved_load = load(7, resolved_hbm, resolved_ref)
+    for j in range(aminos):
+        load(8, outer_hbm, outer_ref.at[:, j])
+
+    def send(src, dst, rsem, g, r):
+        pltpu.make_async_remote_copy(
+            src_ref=src, dst_ref=dst, send_sem=send_s, recv_sem=rsem,
+            device_id={"seq": g, "res": r}, device_id_type=pl.DeviceIdType.MESH,
+        ).start()
 
     def take(view, sem):
         pltpu.make_async_copy(view, view, sem).wait()
 
-    rest, near_rest = pl.ds(0, devices - 1), pl.ds(0, per * (ranks - 1))
-    bias_all, flag_all, right_all = bias_buf.at[rest], flag_buf.at[rest], right_buf.at[rest]
-    left_all = left_buf.at[:, rest]
-    emb_all, out_all = emb_in.at[near_rest], out_ref.at[near_rest]
+    own = pl.ds(rank * per, per)
+    near_all = near.at[:, pl.ds(0, ranks - 1)]
+    side_all = side_buf.at[:, pl.ds(0, devices - 1)]
+    out_all = out_ref.at[pl.ds(0, per * (ranks - 1))]
 
     bias_load.wait()
     lane_head = iota((LANES, HEAD_NUMBER), 0)
@@ -283,44 +277,37 @@
     mask_load.wait()
     flags = dot(mask_ref[...].astype(F32).astype(BF16), one_hot(
         iota((chains, LANES), 0) == iota((chains, LANES), 1)))
-    flag_buf[me] = flags.astype(BF16)
     pair_load.wait()
     pair_value = flat(pair_ref[...].astype(F32))
     own_bias = dot(layer_normalize(pair_value).astype(BF16), wide_w, 1, 1)
     own_bias = jnp.where(
         iota((pairs, LANES), 0) // aminos == iota((pairs, LANES), 1) % pair_rows, own_bias, 0.0)
     own_bias = jnp.sum(own_bias.reshape(pair_rows, aminos, LANES), axis=0)
-    bias_buf[me] = own_bias.astype(BF16)
-    own = pl.ds(rank * per, per)
+    aux = jnp.concatenate([own_bias, flags], axis=1).astype(BF16)
+    for r in range(ranks):
+        pack[r, per] = aux
     emb_load.wait()
-    emb_buf[:, pl.ds(rank, 1)] = emb_in[own][:, None]
+    near[:, pl.ds(rank, 1)] = pack[rank][:, None]
 
     pl.semaphore_wait(barrier, devices - 1)
     for k, g, r in others:
-        send(bias_buf.at[me], bias_buf.at[me], bias_s, bias_r,
-                                where_is(g, r))
-    for k, g, r in others:
         if k < ranks:
-            send(emb_in.at[pl.ds(r * per, per)], emb_buf.at[:, rank],
-                                   emb_s, emb_r, where_is(g, r))
-    for k, g, r in others[::-1]:
-        send(flag_buf.at[me], flag_buf.at[me], flag_s, flag_r,
-                                where_is(g, r))
-
-    heads_q = heads_per * pair_rows
+            send(pack.at[r], near.at[:, rank], near_r, g, r)
+        else:
+            send(pack.at[0, per], far.at[rank], far_r, g, r)
+
     block_mask = (iota((LANES, LANES), 0) % slot // pair_rows
                   == iota((LANES, LANES), 1) // PER_HEAD_DIM)
-    take(emb_all, emb_r)
-    embedding = emb_buf[...].astype(F32).reshape(rows, ROW_FEATURES)
+    take(near_all, near_r)
+    embedding = near[:per].astype(F32).reshape(rows, ROW_FEATURES)
     normed = layer_normalize(embedding).astype(BF16)
     proj_load.wait()
     projected = dot(normed, proj_ref[...])
     queries = (projected[:, :width] * PER_HEAD_DIM ** (-0.5)).astype(BF16)
     keys = projected[:, width:2 * width].astype(BF16)
-    values = projected[:, 2 * width:3 * width].astype(BF16)
-    gating = jax.nn.sigmoid(projected[:, 3 * width:])
-
-    raw = {}
+    value_buf[...] = projected[:, 2 * width:3 * width].astype(BF16)
+    gate_buf[...] = jax.nn.sigmoid(projected[:, 3 * width:])
+
     for b in range(halves):
         cols = slice(b * LANES, (b + 1) * LANES)
         for c in range(per):
@@ -330,33 +317,33 @@
                 spread += [queries[at:at + pair_rows, cols]] * heads_per
             spread = jnp.concatenate(spread, axis=0)
             spread = jnp.where(block_mask, spread, jnp.zeros_like(spread))
-            raw[b, c] = dot(keys[c * full:(c + 1) * full, cols], spread, 1, 1)
-
-    take(flag_all, flag_r)
-    near = flat(flag_buf[pl.ds(group * ranks, ranks)])
+            raw_buf[c * full:(c + 1) * full, cols] = dot(
+                keys[c * full:(c + 1) * full, cols], spread, 1, 1)
+
+    near_aux = flat(near[per])
     pick = one_hot(iota((LANES, per * LANES), 0)
                    == rank * per + iota((LANES, per * LANES), 1) // LANES)
-    key_flags = dot(near, pick)
-    key_mask = (key_flags - 1.0) * 1000000000.0
-    present = jnp.concatenate(
-        [key_flags[:, c * LANES:(c + 1) * LANES] for c in range(per)], axis=0)
-
-    take(bias_all, bias_r)
-    bias = [flat(bias_buf[pl.ds(g * ranks, ranks)]).astype(F32) for g in range(groups)]
+    key_flags = dot(near_aux[:, LANES:], pick)
+    for c in range(per):
+        mask_buf[c * full:(c + 1) * full, :] = key_flags[:, c * LANES:(c + 1) * LANES]
+
+    take(far, far_r)
+    far_aux = flat(far[...])
+    near_bias = near_aux[:, :LANES].astype(F32)
+    far_bias = far_aux[:, :LANES].astype(F32)
     which = iota((full, LANES), 1) // slot
     mixed = []
     for b in range(halves):
         cols = slice(b * LANES, (b + 1) * LANES)
-        tile_bias = bias[b % groups]
-        for s in range(1, groups):
-            tile_bias = jnp.where(which == s, bias[(b - s) % groups], tile_bias)
+        tile_bias = jnp.where((b + which) % groups == group, near_bias, far_bias)
         weights, blocks = [], []
         for c in range(per):
-            scores = raw[b, c] + tile_bias + key_mask[:, c * LANES:(c + 1) * LANES]
+            at = slice(c * full, (c + 1) * full)
+            scores = raw_buf[at, cols] + tile_bias + (mask_buf[at, :] - 1.0) * 1000000000.0
             exponent = jnp.exp(scores - jnp.max(scores, axis=0, keepdims=True))
             total = 1.0 / jnp.sum(exponent, axis=0, keepdims=True)
             weights.append((exponent * total).astype(BF16))
-            own_values = values[c * full:(c + 1) * full, cols]
+            own_values = value_buf[at, cols]
             blocks.append(jnp.concatenate(
                 [own_values if d == c else jnp.zeros_like(own_values) for d in range(per)], axis=1))
         weights = jnp.concatenate(weights, axis=0)
@@ -376,7 +363,7 @@
                 parts.append(part)
         mixed.append(jnp.concatenate(parts, axis=0))
     attended = jnp.concatenate(mixed, axis=1).astype(BF16)
-    gated = (gating * attended.astype(F32)).astype(BF16)
+    gated = (gate_buf[...] * attended.astype(F32)).astype(BF16)
     final_load.wait()
     lr_load.wait()
     updated = (embedding + dot(gated, final_ref[...])).astype(BF16)
@@ -385,35 +372,33 @@
         [lr_ref[:PROJ_FEATURES, :]] * aminos + [lr_ref[PROJ_FEATURES:, :]] * aminos, axis=0)
     sides = dot(normed_out, sides_w, 1, 1)
     two = (rows, 2 * LANES)
-    sides = (sides * jnp.concatenate([present] * 2, axis=1)).astype(BF16)
+    sides = (sides * jnp.concatenate([mask_buf[...]] * 2, axis=1)).astype(BF16)
     sides = jnp.where(iota(two, 1) // PROJ_FEATURES % aminos == iota(two, 0) % aminos,
                       sides, jnp.zeros_like(sides))
     sq = (chains, rows)
     gather = one_hot((iota(sq, 0) // per == iota(sq, 1) % full // aminos)
                      & (iota(sq, 0) % per == iota(sq, 1) // full))
     sides = dot(gather, sides).reshape(ranks, per, 2 * LANES).astype(BF16)
-    left_send[...] = sides[:, :, :LANES]
-    right_send[...] = sides[:, :, LANES:]
-    for k, g, r in others:
-        send(left_send.at[pl.ds(g * quads, quads)], left_buf.at[:, me],
-                                left_s, left_r, where_is(g, r))
-        send(right_send.at[r], right_buf.at[me],
-                                 right_s, right_r, where_is(g, r))
+    left = sides[:, :, :LANES].reshape(groups, quads, per, LANES)
+    right = sides[:, :, LANES:]
+    for r in range(ranks):
+        side_send[:, r, :quads] = left
+    for g in range(groups):
+        side_send[g, :, quads] = right
+    for _, g, r in others:
+        send(side_send.at[g, r], side_buf.at[:, me], side_r, g, r)
     out_send[...] = updated.astype(F32).reshape(per, ranks, aminos, ROW_FEATURES).astype(BF16)
     for k, g, r in others:
         if k < ranks:
-            send(out_send.at[:, r], out_ref.at[own],
-                                   out_s, out_r, where_is(g, r))
-    left_buf[:, pl.ds(me, 1)] = left_send[pl.ds(group * quads, quads)][:, None]
-    right_buf[me] = right_send[rank]
+            send(out_send.at[:, r], out_ref.at[own], out_r, g, r)
+    side_buf[:, pl.ds(me, 1)] = side_send[group, rank][:, None]
     out_ref[own] = out_send[:, pl.ds(rank, 1)].reshape(per, aminos, ROW_FEATURES)
 
     at = (pairs, full)
     row_pick = iota(at, 1) == group * pair_rows + iota(at, 0) // aminos
     col_pick = iota(at, 1) == rank * aminos + iota(at, 0) % aminos
     both = jnp.zeros((pairs, LANES), F32)
-    for g in range(groups):
-        seen = flat(flag_buf[pl.ds(g * ranks, ranks)])
+    for seen in (near_aux[:, LANES:], far_aux[:, LANES:]):
         both = both + dot(one_hot(row_pick), seen) * dot(one_hot(col_pick), seen)
     counts = jnp.sum(both, axis=1, keepdims=True)
     resolved_load.wait()
@@ -421,33 +406,25 @@
     scale = jnp.sum(jnp.where(row_pick, resolved, 0.0), axis=1, keepdims=True) * jnp.sum(
         jnp.where(col_pick, resolved, 0.0), axis=1, keepdims=True) / counts
     scale = jnp.broadcast_to(scale, (pairs, LANES))
-    outer_load.wait()
+    take(outer_ref, load_s.at[8])
     block = iota((pair_rows, LANES), 1) // PROJ_FEATURES
-    take(right_all, right_r)
-    take(left_all, left_r)
-    right_rows = flat(right_buf[...])
+    take(side_all, side_r)
+    right_rows = flat(side_buf[quads])
     for q in range(quads):
-        product_buf[q * LANES:(q + 1) * LANES, :] = dot(flat(left_buf[q]), right_rows, 0, 0)
-    for c in range(0, PROJ_FEATURES, aminos):
-        slabs = [product_buf[pl.ds(c + x, pair_rows, stride=PROJ_FEATURES), :]
-                 for x in range(aminos)]
-        for j in range(aminos):
-            turned = jnp.zeros((pair_rows, LANES), F32)
-            for x in range(aminos):
-                shift = (x - j) % aminos * PROJ_FEATURES
-                moved = pltpu.roll(slabs[x], shift, 1) if shift else slabs[x]
-                turned = jnp.where(block == x, moved, turned)
-            lhs_buf[j * pair_rows:(j + 1) * pair_rows,
-                    c * PROJ_FEATURES:c * PROJ_FEATURES + LANES] = turned.astype(BF16)
-    outer = dot(lhs_buf[...], outer_ref[...])
+        product_buf[q * LANES:(q + 1) * LANES, :] = dot(flat(side_buf[q]), right_rows, 0, 0)
+    parts = []
+    for c in range(PROJ_FEATURES):
+        slab = product_buf[pl.ds(c, pair_rows, stride=PROJ_FEATURES), :].astype(BF16)
+        parts.append(jnp.concatenate(
+            [jnp.where(block == j, slab, jnp.zeros_like(slab)) for j in range(aminos)], axis=0))
+    outer = dot(jnp.concatenate(parts, axis=1), flat(outer_ref[...].reshape(-1, CZ)))
     for j in range(aminos):
         turn_buf[pl.ds(j, pair_rows, stride=aminos), :] = outer[j * pair_rows:(j + 1) * pair_rows]
     result = pair_value + scale * turn_buf[...]
     pair_out_ref[...] = result.reshape(pair_rows, aminos, CZ).astype(BF16)
     take(out_all, out_r)
-    for view, sem in ((bias_all, bias_s), (emb_all, emb_s), (flag_all, flag_s),
-                      (left_all, left_s), (right_all, right_s), (out_all, out_s)):
-        take(view, sem)
+    for view in (near_all, far, side_all, out_all):
+        take(view, send_s)
 
 
 def write_kernel(out_ref, pair_ref, out_hbm, pair_hbm, sem):
@@ -467,8 +444,8 @@
     pair_rows = pair.shape[0]
     quads = pair_rows // aminos
     devices = groups * ranks
-    operands = (emb, mask.T, resolved.reshape(1, -1), pair, args[4], args[5].T, args[6],
-                args[7].T, args[8])
+    operands = (emb.reshape(ranks, per, aminos, ROW_FEATURES), mask.T, resolved.reshape(1, -1), pair, args[4], args[5].T, args[6],
+                args[7].T, args[8].reshape(PROJ_FEATURES, PROJ_FEATURES, CZ))
     vmem = pl.BlockSpec(memory_space=pltpu.VMEM)
     whole = pl.BlockSpec(memory_space=pl.ANY)
     dma = pltpu.SemaphoreType.DMA
@@ -477,20 +454,23 @@
         out_shape=(pltpu.VMEM(emb.shape, BF16), pltpu.VMEM(pair.shape, BF16)),
         in_specs=[whole] * len(operands),
         out_specs=(vmem, vmem),
-        scratch_shapes=[pltpu.VMEM(x.shape, x.dtype) for x in operands] + [
+        scratch_shapes=[
+            pltpu.VMEM((ranks, per + 1, aminos, ROW_FEATURES), BF16),
+            pltpu.VMEM((per + 1, ranks, aminos, ROW_FEATURES), BF16),
+            pltpu.VMEM((ranks, aminos, ROW_FEATURES), BF16),
+        ] + [pltpu.VMEM(x.shape, x.dtype) for x in operands[1:8]] + [
+            pltpu.VMEM((PROJ_FEATURES, aminos, PROJ_FEATURES, CZ), BF16),
+            pltpu.VMEM((groups, ranks, quads + 1, per, LANES), BF16),
+            pltpu.VMEM((quads + 1, devices, per, LANES), BF16),
             pltpu.VMEM((per, ranks, aminos, ROW_FEATURES), BF16),
-            pltpu.VMEM((devices, aminos, LANES), BF16),
-            pltpu.VMEM((devices, aminos, LANES), BF16),
-            pltpu.VMEM((ranks, per, LANES), BF16),
-            pltpu.VMEM((ranks, per, LANES), BF16),
-            pltpu.VMEM((quads, devices, per, LANES), BF16),
-            pltpu.VMEM((devices, per, LANES), BF16),
-            pltpu.VMEM((per, ranks, aminos, ROW_FEATURES), BF16),
+            pltpu.VMEM((chains * aminos, ROW_FEATURES), F32),
+            pltpu.VMEM((chains * aminos, LANES), F32),
+            pltpu.VMEM((chains * aminos, ROW_FEATURES), F32),
+            pltpu.VMEM((chains * aminos, ROW_FEATURES), BF16),
             pltpu.VMEM((pair_rows * PROJ_FEATURES, LANES), F32),
-            pltpu.VMEM((pair_rows * aminos, PROJ_FEATURES * PROJ_FEATURES), BF16),
             pltpu.VMEM((pair_rows * aminos, CZ), F32),
-            dma((len(operands),)),
-        ] + [dma] * 12,
+            dma((len(operands),)), dma, dma, dma, dma, dma,
+        ],
         compiler_params=pltpu.CompilerParams(collective_id=0, has_side_effects=True),
     )(*operands)
     return pl.pallas_call(

time: 18.9 us -> 18.2 us (0.963)
  Pallas kernels: 18.1 us -> 17.4 us
    pallas_call x1, Pallas kernels: 17.5 us -> 16.8 us  [fused(): pl.pallas_call(functools.partial(fused_kernel, groups, ranks, per, aminos...]
where the time goes in v2:
time: 18.2 us; the launch traced here: 18.1 us
  Pallas kernels  17.4 us (96%)
  between operations  0.64 us (4%)
    pallas_call x1, Pallas kernels, fused(): pl.pallas_call(functools.partial(fused_kernel, groups, ranks, per, aminos...  16.8 us
    pallas_call x1, Pallas kernels, fused(): pl.pallas_call(write_kernel, out_shape=(jax.ShapeDtypeStruct(emb.shape, B...  0.65 us

profile of v2, /device:TPU:0, one launch (start us, length us, event | category | flops | bytes accessed | tf_op | source)
XLA Modules:
  0.0 18.1 jit_solution(13514273227528450160)
XLA Ops:
  0.6 16.8 %shard_map.104 = (bf16[32,4,256]{2,1,0:T(4,128)(2,1)S(1)}, bf16[16,4,128]{2,1,0:T(4,128)(2,1)S(1)}) custom-call(bf16[8,4,4,256]{3,2,1,0:T(4,128)(2,1)} %bitcast.7, s32[4,32]{1,0:T(4,128)} %bitcast.9, s32[1,32]{1,0:T(1,128)} %bitcast.11, bf16[16,4,128]{2,1,0:T(4,128)(2,1)} %pair_hbm.1, bf16[256,1024]{1,0:T(8,128)(2,1)} %proj_hbm.1, bf16[8,128]{1,0:T(8,128)(2,1)} %bitcast.10, ...), custom_call_target="tpu_custom_call" | custom-call | tf_op jit(solution)/shard_map/pallas_call | solution.py:452
  17.4 0.7 %shard_map.105 = (bf16[32,4,256]{2,1,0:T(4,128)(2,1)}, bf16[16,4,128]{2,1,0:T(4,128)(2,1)}) custom-call(bf16[32,4,256]{2,1,0:T(4,128)(2,1)S(1)} %get-tuple-element.4.out_ref, bf16[16,4,128]{2,1,0:T(4,128)(2,1)S(1)} %get-tuple-element.5.pair_ref), custom_call_target="tpu_custom_call" | custom-call | tf_op jit(solution)/shard_map/pallas_call | solution.py:476

commit v3 on v2

--- a/solution.py
+++ b/solution.py
@@ -198,13 +198,30 @@
     return block.reshape(-1, block.shape[-1])
 
 
+def turn_blocks(slabs):
+    count = len(slabs)
+    size = LANES // count
+    lane = iota(slabs[0].shape, 1) // size
+    slabs = list(slabs)
+    half = count // 2
+    while half:
+        low = lane // half % 2 == 0
+        for x in range(count):
+            if x // half % 2 == 0:
+                a, b = slabs[x], slabs[x + half]
+                slabs[x] = jnp.where(low, a, pltpu.roll(b, half * size, 1))
+                slabs[x + half] = jnp.where(low, pltpu.roll(a, LANES - half * size, 1), b)
+        half //= 2
+    return slabs
+
+
 def fused_kernel(
     groups, ranks, per, aminos,
     emb_hbm, mask_hbm, resolved_hbm, pair_hbm, proj_hbm, bias_hbm, final_hbm, lr_hbm, outer_hbm,
     out_ref, pair_out_ref,
     pack, near, far, mask_ref, resolved_ref, pair_ref, proj_ref, bias_w_ref, final_ref, lr_ref,
-    outer_ref, side_send, side_buf, out_send, raw_buf, mask_buf, gate_buf, value_buf,
-    product_buf, turn_buf, load_s, send_s, near_r, far_r, side_r, out_r,
+    outer_ref, side_send, side_buf, out_send, raw_buf, mask_buf, keep_buf, gate_buf, value_buf,
+    pick_ref, gather_ref, sides_w_ref, turn_buf, load_s, send_s, near_r, far_r, side_r, out_r,
 ):
     devices = groups * ranks
     chains = per * ranks
@@ -217,6 +234,8 @@
     halves = width // LANES
     heads_per = LANES // PER_HEAD_DIM
     slot = LANES // groups
+    folds = 8 // aminos
+    cores = math.gcd(2, ranks)
     group = lax.axis_index("seq")
     rank = lax.axis_index("res")
     me = group * ranks + rank
@@ -253,8 +272,8 @@
     final_load = load(5, final_hbm, final_ref)
     lr_load = load(6, lr_hbm, lr_ref)
     resolved_load = load(7, resolved_hbm, resolved_ref)
-    for j in range(aminos):
-        load(8, outer_hbm, outer_ref.at[:, j])
+    for x in range(folds):
+        load(8, outer_hbm.at[:, x], outer_ref.at[:, :, pl.ds(x * CZ, CZ)])
 
     def send(src, dst, rsem, g, r):
         pltpu.make_async_remote_copy(
@@ -296,12 +315,26 @@
         else:
             send(pack.at[0, per], far.at[rank], far_r, g, r)
 
+    for copy in (proj_load, final_load, lr_load, resolved_load):
+        copy.wait()
     block_mask = (iota((LANES, LANES), 0) % slot // pair_rows
                   == iota((LANES, LANES), 1) // PER_HEAD_DIM)
+    at = (LANES, per * LANES)
+    pick_ref[...] = one_hot(iota(at, 0) == rank * per + iota(at, 1) // LANES)
+    at = (chains, rows)
+    gather_ref[...] = one_hot((iota(at, 0) // per == iota(at, 1) % full // aminos)
+                              & (iota(at, 0) % per == iota(at, 1) // full))
+    at = (2 * LANES, 2 * PROJ_FEATURES)
+    left_row, right_row = iota(at, 0) // aminos, PROJ_FEATURES + iota(at, 0) % PROJ_FEATURES
+    sides_w_ref[...] = dot(one_hot(
+        jnp.where(iota(at, 0) < LANES, left_row, right_row) == iota(at, 1)), lr_ref[...]).astype(BF16)
+    two = (rows, 2 * LANES)
+    amino = jnp.where(iota(two, 1) < LANES, iota(two, 1) % aminos,
+                      iota(two, 1) % LANES // PROJ_FEATURES)
+    keep_buf[...] = jnp.where(amino == iota(two, 0) % aminos, 1.0, 0.0)
     take(near_all, near_r)
     embedding = near[:per].astype(F32).reshape(rows, ROW_FEATURES)
     normed = layer_normalize(embedding).astype(BF16)
-    proj_load.wait()
     projected = dot(normed, proj_ref[...])
     queries = (projected[:, :width] * PER_HEAD_DIM ** (-0.5)).astype(BF16)
     keys = projected[:, width:2 * width].astype(BF16)
@@ -321,12 +354,12 @@
                 keys[c * full:(c + 1) * full, cols], spread, 1, 1)
 
     near_aux = flat(near[per])
-    pick = one_hot(iota((LANES, per * LANES), 0)
-                   == rank * per + iota((LANES, per * LANES), 1) // LANES)
-    key_flags = dot(near_aux[:, LANES:], pick)
+    key_flags = dot(near_aux[:, LANES:], pick_ref[...])
     for c in range(per):
-        mask_buf[c * full:(c + 1) * full, :] = key_flags[:, c * LANES:(c + 1) * LANES]
-
+        at = slice(c * full, (c + 1) * full)
+        present = key_flags[:, c * LANES:(c + 1) * LANES]
+        mask_buf[at, :] = (present - 1.0) * 1000000000.0
+        keep_buf[at, :] = keep_buf[at, :] * jnp.concatenate([present] * 2, axis=1)
     take(far, far_r)
     far_aux = flat(far[...])
     near_bias = near_aux[:, :LANES].astype(F32)
@@ -339,7 +372,7 @@
         weights, blocks = [], []
         for c in range(per):
             at = slice(c * full, (c + 1) * full)
-            scores = raw_buf[at, cols] + tile_bias + (mask_buf[at, :] - 1.0) * 1000000000.0
+            scores = raw_buf[at, cols] + tile_bias + mask_buf[at, :]
             exponent = jnp.exp(scores - jnp.max(scores, axis=0, keepdims=True))
             total = 1.0 / jnp.sum(exponent, axis=0, keepdims=True)
             weights.append((exponent * total).astype(BF16))
@@ -364,33 +397,28 @@
         mixed.append(jnp.concatenate(parts, axis=0))
     attended = jnp.concatenate(mixed, axis=1).astype(BF16)
     gated = (gate_buf[...] * attended.astype(F32)).astype(BF16)
-    final_load.wait()
-    lr_load.wait()
     updated = (embedding + dot(gated, final_ref[...])).astype(BF16)
+    out_send[...] = updated.astype(F32).reshape(per, ranks, aminos, ROW_FEATURES).astype(BF16)
     normed_out = layer_normalize(updated).astype(BF16)
-    sides_w = jnp.concatenate(
-        [lr_ref[:PROJ_FEATURES, :]] * aminos + [lr_ref[PROJ_FEATURES:, :]] * aminos, axis=0)
-    sides = dot(normed_out, sides_w, 1, 1)
-    two = (rows, 2 * LANES)
-    sides = (sides * jnp.concatenate([mask_buf[...]] * 2, axis=1)).astype(BF16)
-    sides = jnp.where(iota(two, 1) // PROJ_FEATURES % aminos == iota(two, 0) % aminos,
-                      sides, jnp.zeros_like(sides))
-    sq = (chains, rows)
-    gather = one_hot((iota(sq, 0) // per == iota(sq, 1) % full // aminos)
-                     & (iota(sq, 0) % per == iota(sq, 1) // full))
-    sides = dot(gather, sides).reshape(ranks, per, 2 * LANES).astype(BF16)
+    sides = (dot(normed_out, sides_w_ref[...], 1, 1) * keep_buf[...]).astype(BF16)
+    sides = dot(gather_ref[...], sides).reshape(ranks, per, 2 * LANES).astype(BF16)
     left = sides[:, :, :LANES].reshape(groups, quads, per, LANES)
     right = sides[:, :, LANES:]
     for r in range(ranks):
         side_send[:, r, :quads] = left
     for g in range(groups):
         side_send[g, :, quads] = right
-    for _, g, r in others:
+    place = rank // cores * groups * cores + group * cores + lax.rem(rank, cores)
+    for n in range(devices - 1):
+        at = n + lax.div(n - place + devices, devices)
+        g = lax.rem(lax.div(at, cores), groups)
+        r = lax.div(at, groups * cores) * cores + lax.rem(at, cores)
         send(side_send.at[g, r], side_buf.at[:, me], side_r, g, r)
-    out_send[...] = updated.astype(F32).reshape(per, ranks, aminos, ROW_FEATURES).astype(BF16)
-    for k, g, r in others:
-        if k < ranks:
-            send(out_send.at[:, r], out_ref.at[own], out_r, g, r)
+        if n % (groups * cores) == cores - 1:
+            for m in range(n // groups // cores * cores, n // groups // cores * cores + cores):
+                if m < ranks - 1:
+                    r = m + lax.div(m - rank + ranks, ranks)
+                    send(out_send.at[:, r], out_ref.at[own], out_r, group, r)
     side_buf[:, pl.ds(me, 1)] = side_send[group, rank][:, None]
     out_ref[own] = out_send[:, pl.ds(rank, 1)].reshape(per, aminos, ROW_FEATURES)
 
@@ -401,25 +429,31 @@
     for seen in (near_aux[:, LANES:], far_aux[:, LANES:]):
         both = both + dot(one_hot(row_pick), seen) * dot(one_hot(col_pick), seen)
     counts = jnp.sum(both, axis=1, keepdims=True)
-    resolved_load.wait()
     resolved = jnp.broadcast_to(resolved_ref[...].astype(F32), at)
     scale = jnp.sum(jnp.where(row_pick, resolved, 0.0), axis=1, keepdims=True) * jnp.sum(
         jnp.where(col_pick, resolved, 0.0), axis=1, keepdims=True) / counts
     scale = jnp.broadcast_to(scale, (pairs, LANES))
     take(outer_ref, load_s.at[8])
-    block = iota((pair_rows, LANES), 1) // PROJ_FEATURES
     take(side_all, side_r)
     right_rows = flat(side_buf[quads])
-    for q in range(quads):
-        product_buf[q * LANES:(q + 1) * LANES, :] = dot(flat(side_buf[q]), right_rows, 0, 0)
+    products = [dot(flat(side_buf[q]), right_rows, 0, 0) for q in range(quads)]
     parts = []
-    for c in range(PROJ_FEATURES):
-        slab = product_buf[pl.ds(c, pair_rows, stride=PROJ_FEATURES), :].astype(BF16)
-        parts.append(jnp.concatenate(
-            [jnp.where(block == j, slab, jnp.zeros_like(slab)) for j in range(aminos)], axis=0))
-    outer = dot(jnp.concatenate(parts, axis=1), flat(outer_ref[...].reshape(-1, CZ)))
+    step = folds * aminos
+    for c in range(0, PROJ_FEATURES // folds, aminos):
+        slabs = []
+        for x in range(c, c + aminos):
+            slab = [product[x * step:(x + 1) * step] for product in products]
+            slabs.append(jnp.concatenate(slab, axis=0))
+        parts.append(jnp.concatenate(turn_blocks(slabs), axis=0).astype(BF16))
+    outer = dot(jnp.concatenate(parts, axis=1), outer_ref[...].reshape(-1, folds * CZ))
     for j in range(aminos):
-        turn_buf[pl.ds(j, pair_rows, stride=aminos), :] = outer[j * pair_rows:(j + 1) * pair_rows]
+        for q in range(quads):
+            base = (j * quads + q) * folds * aminos
+            total = outer[base:base + aminos, :CZ]
+            for x in range(1, folds):
+                row = base + x * aminos
+                total = total + outer[row:row + aminos, x * CZ:(x + 1) * CZ]
+            turn_buf[pl.ds(q * aminos * aminos + j, aminos, stride=aminos), :] = total
     result = pair_value + scale * turn_buf[...]
     pair_out_ref[...] = result.reshape(pair_rows, aminos, CZ).astype(BF16)
     take(out_all, out_r)
@@ -444,8 +478,9 @@
     pair_rows = pair.shape[0]
     quads = pair_rows // aminos
     devices = groups * ranks
+    folds = 8 // aminos
     operands = (emb.reshape(ranks, per, aminos, ROW_FEATURES), mask.T, resolved.reshape(1, -1), pair, args[4], args[5].T, args[6],
-                args[7].T, args[8].reshape(PROJ_FEATURES, PROJ_FEATURES, CZ))
+                args[7].T, args[8].reshape(PROJ_FEATURES // folds, folds, PROJ_FEATURES, CZ))
     vmem = pl.BlockSpec(memory_space=pltpu.VMEM)
     whole = pl.BlockSpec(memory_space=pl.ANY)
     dma = pltpu.SemaphoreType.DMA
@@ -459,15 +494,18 @@
             pltpu.VMEM((per + 1, ranks, aminos, ROW_FEATURES), BF16),
             pltpu.VMEM((ranks, aminos, ROW_FEATURES), BF16),
         ] + [pltpu.VMEM(x.shape, x.dtype) for x in operands[1:8]] + [
-            pltpu.VMEM((PROJ_FEATURES, aminos, PROJ_FEATURES, CZ), BF16),
+            pltpu.VMEM((PROJ_FEATURES // folds, PROJ_FEATURES, folds * CZ), BF16),
             pltpu.VMEM((groups, ranks, quads + 1, per, LANES), BF16),
             pltpu.VMEM((quads + 1, devices, per, LANES), BF16),
             pltpu.VMEM((per, ranks, aminos, ROW_FEATURES), BF16),
             pltpu.VMEM((chains * aminos, ROW_FEATURES), F32),
             pltpu.VMEM((chains * aminos, LANES), F32),
+            pltpu.VMEM((chains * aminos, 2 * LANES), F32),
             pltpu.VMEM((chains * aminos, ROW_FEATURES), F32),
             pltpu.VMEM((chains * aminos, ROW_FEATURES), BF16),
-            pltpu.VMEM((pair_rows * PROJ_FEATURES, LANES), F32),
+            pltpu.VMEM((LANES, per * LANES), BF16),
+            pltpu.VMEM((chains, chains * aminos), BF16),
+            pltpu.VMEM((2 * LANES, ROW_FEATURES), BF16),
             pltpu.VMEM((pair_rows * aminos, CZ), F32),
             dma((len(operands),)), dma, dma, dma, dma, dma,
         ],

time: 18.2 us -> 17.6 us (0.967)
  Pallas kernels: 17.4 us -> 16.8 us
    pallas_call x1, Pallas kernels: 16.8 us -> 16.1 us  [fused(): pl.pallas_call(functools.partial(fused_kernel, groups, ranks, per, aminos...]
where the time goes in v3:
time: 17.6 us; the launch traced here: 17.4 us
  Pallas kernels  16.8 us (95%)
  between operations  0.64 us (4%)
    pallas_call x1, Pallas kernels, fused(): pl.pallas_call(functools.partial(fused_kernel, groups, ranks, per, aminos...  16.1 us
    pallas_call x1, Pallas kernels, fused(): pl.pallas_call(write_kernel, out_shape=(jax.ShapeDtypeStruct(emb.shape, B...  0.65 us

profile of v3, /device:TPU:0, one launch (start us, length us, event | category | flops | bytes accessed | tf_op | source)
XLA Modules:
  0.0 17.4 jit_solution(11423483985273613039)
XLA Ops:
  0.6 16.1 %shard_map.104 = (bf16[32,4,256]{2,1,0:T(4,128)(2,1)S(1)}, bf16[16,4,128]{2,1,0:T(4,128)(2,1)S(1)}) custom-call(bf16[8,4,4,256]{3,2,1,0:T(4,128)(2,1)} %bitcast.7, s32[4,32]{1,0:T(4,128)} %bitcast.9, s32[1,32]{1,0:T(1,128)} %bitcast.11, bf16[16,4,128]{2,1,0:T(4,128)(2,1)} %pair_hbm.1, bf16[256,1024]{1,0:T(8,128)(2,1)} %proj_hbm.1, bf16[8,128]{1,0:T(8,128)(2,1)} %bitcast.10, ...), custom_call_target="tpu_custom_call" | custom-call | tf_op jit(solution)/shard_map/pallas_call | solution.py:487
  16.7 0.7 %shard_map.105 = (bf16[32,4,256]{2,1,0:T(4,128)(2,1)}, bf16[16,4,128]{2,1,0:T(4,128)(2,1)}) custom-call(bf16[32,4,256]{2,1,0:T(4,128)(2,1)S(1)} %get-tuple-element.4.out_ref, bf16[16,4,128]{2,1,0:T(4,128)(2,1)S(1)} %get-tuple-element.5.pair_ref), custom_call_target="tpu_custom_call" | custom-call | tf_op jit(solution)/shard_map/pallas_call | solution.py:514

commit v4 on v3

--- a/solution.py
+++ b/solution.py
@@ -240,18 +240,24 @@
     rank = lax.axis_index("res")
     me = group * ranks + rank
 
+    chip, core = rank // cores, rank % cores
+
     def flip(k):
         peer = 0
-        for bit in range(ranks.bit_length() - 1):
-            digit = rank // (1 << bit) % 2
+        for bit in range((ranks // cores).bit_length() - 1):
+            digit = chip // (1 << bit) % 2
             peer = peer + (1 << bit) * (1 - digit if k >> bit & 1 else digit)
         return peer
 
     others = []
     for shift in range(groups - 1, -1, -1):
-        for k in range(ranks - 1, -1, -1):
-            if shift or k:
-                others.append((shift * ranks + k, lax.rem(group + shift, groups), flip(k)))
+        g = lax.rem(group + shift, groups)
+        for k in range(ranks // cores - 1, -1, -1):
+            for x in range(cores):
+                if shift or k:
+                    others.append((shift, g, flip(k) * cores + x))
+    for x in range(1, cores):
+        others.append((0, group, chip * cores + lax.rem(core + x, cores)))
 
     barrier = pltpu.get_barrier_semaphore()
     for _, g, r in others:
@@ -269,11 +275,11 @@
     bias_load = load(2, bias_hbm, bias_w_ref)
     mask_load = load(3, mask_hbm, mask_ref)
     proj_load = load(4, proj_hbm, proj_ref)
-    final_load = load(5, final_hbm, final_ref)
-    lr_load = load(6, lr_hbm, lr_ref)
-    resolved_load = load(7, resolved_hbm, resolved_ref)
+    final_load = load(4, final_hbm, final_ref)
+    lr_load = load(4, lr_hbm, lr_ref)
+    resolved_load = load(4, resolved_hbm, resolved_ref)
     for x in range(folds):
-        load(8, outer_hbm.at[:, x], outer_ref.at[:, :, pl.ds(x * CZ, CZ)])
+        load(5, outer_hbm.at[:, x], outer_ref.at[:, :, pl.ds(x * CZ, CZ)])
 
     def send(src, dst, rsem, g, r):
         pltpu.make_async_remote_copy(
@@ -309,11 +315,11 @@
     near[:, pl.ds(rank, 1)] = pack[rank][:, None]
 
     pl.semaphore_wait(barrier, devices - 1)
-    for k, g, r in others:
-        if k < ranks:
+    for shift, g, r in others:
+        if shift:
+            send(pack.at[0, per], far.at[rank], far_r, g, r)
+        else:
             send(pack.at[r], near.at[:, rank], near_r, g, r)
-        else:
-            send(pack.at[0, per], far.at[rank], far_r, g, r)
 
     for copy in (proj_load, final_load, lr_load, resolved_load):
         copy.wait()
@@ -404,16 +410,21 @@
     sides = dot(gather_ref[...], sides).reshape(ranks, per, 2 * LANES).astype(BF16)
     left = sides[:, :, :LANES].reshape(groups, quads, per, LANES)
     right = sides[:, :, LANES:]
-    for r in range(ranks):
-        side_send[:, r, :quads] = left
-    for g in range(groups):
-        side_send[g, :, quads] = right
+    def fill(start, stop):
+        for r in range(start, stop):
+            side_send[:, r, :quads] = left
+        for g in range(groups):
+            side_send[g, start:stop, quads] = right[start:stop]
+
+    fill(0, 2 * cores)
     place = rank // cores * groups * cores + group * cores + lax.rem(rank, cores)
     for n in range(devices - 1):
         at = n + lax.div(n - place + devices, devices)
         g = lax.rem(lax.div(at, cores), groups)
         r = lax.div(at, groups * cores) * cores + lax.rem(at, cores)
         send(side_send.at[g, r], side_buf.at[:, me], side_r, g, r)
+        if n == cores - 1:
+            fill(2 * cores, ranks)
         if n % (groups * cores) == cores - 1:
             for m in range(n // groups // cores * cores, n // groups // cores * cores + cores):
                 if m < ranks - 1:
@@ -433,7 +444,7 @@
     scale = jnp.sum(jnp.where(row_pick, resolved, 0.0), axis=1, keepdims=True) * jnp.sum(
         jnp.where(col_pick, resolved, 0.0), axis=1, keepdims=True) / counts
     scale = jnp.broadcast_to(scale, (pairs, LANES))
-    take(outer_ref, load_s.at[8])
+    take(outer_ref, load_s.at[5])
     take(side_all, side_r)
     right_rows = flat(side_buf[quads])
     products = [dot(flat(side_buf[q]), right_rows, 0, 0) for q in range(quads)]
@@ -443,8 +454,8 @@
         slabs = []
         for x in range(c, c + aminos):
             slab = [product[x * step:(x + 1) * step] for product in products]
-            slabs.append(jnp.concatenate(slab, axis=0))
-        parts.append(jnp.concatenate(turn_blocks(slabs), axis=0).astype(BF16))
+            slabs.append(jnp.concatenate(slab, axis=0).astype(BF16))
+        parts.append(jnp.concatenate(turn_blocks(slabs), axis=0))
     outer = dot(jnp.concatenate(parts, axis=1), outer_ref[...].reshape(-1, folds * CZ))
     for j in range(aminos):
         for q in range(quads):
@@ -507,7 +518,7 @@
             pltpu.VMEM((chains, chains * aminos), BF16),
             pltpu.VMEM((2 * LANES, ROW_FEATURES), BF16),
             pltpu.VMEM((pair_rows * aminos, CZ), F32),
-            dma((len(operands),)), dma, dma, dma, dma, dma,
+            dma((6,)), dma, dma, dma, dma, dma,
         ],
         compiler_params=pltpu.CompilerParams(collective_id=0, has_side_effects=True),
     )(*operands)

time: 17.6 us -> 17.5 us (level)
  no operation moved by 1% of the time
where the time goes in v4:
time: 17.5 us; the launch traced here: 17.3 us
  Pallas kernels  16.7 us (95%)
  between operations  0.64 us (4%)
    pallas_call x1, Pallas kernels, fused(): pl.pallas_call(functools.partial(fused_kernel, groups, ranks, per, aminos...  16 us
    pallas_call x1, Pallas kernels, fused(): pl.pallas_call(write_kernel, out_shape=(jax.ShapeDtypeStruct(emb.shape, B...  0.65 us

profile of v4, /device:TPU:0, one launch (start us, length us, event | category | flops | bytes accessed | tf_op | source)
XLA Modules:
  0.0 17.3 jit_solution(12684996456208855066)
XLA Ops:
  0.6 16.0 %shard_map.104 = (bf16[32,4,256]{2,1,0:T(4,128)(2,1)S(1)}, bf16[16,4,128]{2,1,0:T(4,128)(2,1)S(1)}) custom-call(bf16[8,4,4,256]{3,2,1,0:T(4,128)(2,1)} %bitcast.7, s32[4,32]{1,0:T(4,128)} %bitcast.9, s32[1,32]{1,0:T(1,128)} %bitcast.11, bf16[16,4,128]{2,1,0:T(4,128)(2,1)} %pair_hbm.1, bf16[256,1024]{1,0:T(8,128)(2,1)} %proj_hbm.1, bf16[8,128]{1,0:T(8,128)(2,1)} %bitcast.10, ...), custom_call_target="tpu_custom_call" | custom-call | tf_op jit(solution)/shard_map/pallas_call | solution.py:498
  16.6 0.7 %shard_map.105 = (bf16[32,4,256]{2,1,0:T(4,128)(2,1)}, bf16[16,4,128]{2,1,0:T(4,128)(2,1)}) custom-call(bf16[32,4,256]{2,1,0:T(4,128)(2,1)S(1)} %get-tuple-element.4.out_ref, bf16[16,4,128]{2,1,0:T(4,128)(2,1)S(1)} %get-tuple-element.5.pair_ref), custom_call_target="tpu_custom_call" | custom-call | tf_op jit(solution)/shard_map/pallas_call | solution.py:525

commit v5 on v4

--- a/solution.py
+++ b/solution.py
@@ -221,7 +221,7 @@
     out_ref, pair_out_ref,
     pack, near, far, mask_ref, resolved_ref, pair_ref, proj_ref, bias_w_ref, final_ref, lr_ref,
     outer_ref, side_send, side_buf, out_send, raw_buf, mask_buf, keep_buf, gate_buf, value_buf,
-    pick_ref, gather_ref, sides_w_ref, turn_buf, load_s, send_s, near_r, far_r, side_r, out_r,
+    pick_ref, gather_ref, sides_w_ref, turn_buf, load_s, send_s, near_r, far_r, flag_r, side_r, out_r,
 ):
     devices = groups * ranks
     chains = per * ranks
@@ -291,6 +291,7 @@
         pltpu.make_async_copy(view, view, sem).wait()
 
     own = pl.ds(rank * per, per)
+    low, high = pl.ds(0, LANES), pl.ds(LANES, LANES)
     near_all = near.at[:, pl.ds(0, ranks - 1)]
     side_all = side_buf.at[:, pl.ds(0, devices - 1)]
     out_all = out_ref.at[pl.ds(0, per * (ranks - 1))]
@@ -317,10 +318,9 @@
     pl.semaphore_wait(barrier, devices - 1)
     for shift, g, r in others:
         if shift:
-            send(pack.at[0, per], far.at[rank], far_r, g, r)
+            send(pack.at[0, per, :, low], far.at[rank, :, low], far_r, g, r)
         else:
             send(pack.at[r], near.at[:, rank], near_r, g, r)
-
     for copy in (proj_load, final_load, lr_load, resolved_load):
         copy.wait()
     block_mask = (iota((LANES, LANES), 0) % slot // pair_rows
@@ -338,6 +338,9 @@
     amino = jnp.where(iota(two, 1) < LANES, iota(two, 1) % aminos,
                       iota(two, 1) % LANES // PROJ_FEATURES)
     keep_buf[...] = jnp.where(amino == iota(two, 0) % aminos, 1.0, 0.0)
+    for shift, g, r in others:
+        if shift:
+            send(pack.at[0, per, :, high], far.at[rank, :, high], flag_r, g, r)
     take(near_all, near_r)
     embedding = near[:per].astype(F32).reshape(rows, ROW_FEATURES)
     normed = layer_normalize(embedding).astype(BF16)
@@ -366,10 +369,9 @@
         present = key_flags[:, c * LANES:(c + 1) * LANES]
         mask_buf[at, :] = (present - 1.0) * 1000000000.0
         keep_buf[at, :] = keep_buf[at, :] * jnp.concatenate([present] * 2, axis=1)
-    take(far, far_r)
-    far_aux = flat(far[...])
+    take(far.at[:, :, low], far_r)
+    far_bias = flat(far[:, :, :LANES]).astype(F32)
     near_bias = near_aux[:, :LANES].astype(F32)
-    far_bias = far_aux[:, :LANES].astype(F32)
     which = iota((full, LANES), 1) // slot
     mixed = []
     for b in range(halves):
@@ -437,7 +439,8 @@
     row_pick = iota(at, 1) == group * pair_rows + iota(at, 0) // aminos
     col_pick = iota(at, 1) == rank * aminos + iota(at, 0) % aminos
     both = jnp.zeros((pairs, LANES), F32)
-    for seen in (near_aux[:, LANES:], far_aux[:, LANES:]):
+    take(far.at[:, :, high], flag_r)
+    for seen in (near_aux[:, LANES:], flat(far[:, :, LANES:])):
         both = both + dot(one_hot(row_pick), seen) * dot(one_hot(col_pick), seen)
     counts = jnp.sum(both, axis=1, keepdims=True)
     resolved = jnp.broadcast_to(resolved_ref[...].astype(F32), at)
@@ -518,7 +521,7 @@
             pltpu.VMEM((chains, chains * aminos), BF16),
             pltpu.VMEM((2 * LANES, ROW_FEATURES), BF16),
             pltpu.VMEM((pair_rows * aminos, CZ), F32),
-            dma((6,)), dma, dma, dma, dma, dma,
+            dma((6,)), dma, dma, dma, dma, dma, dma,
         ],
         compiler_params=pltpu.CompilerParams(collective_id=0, has_side_effects=True),
     )(*operands)

time: 17.5 us -> 17.5 us (level)
  no operation moved by 1% of the time
where the time goes in v5:
time: 17.5 us; the launch traced here: 17.3 us
  Pallas kernels  16.7 us (95%)
  between operations  0.64 us (4%)
    pallas_call x1, Pallas kernels, fused(): pl.pallas_call(functools.partial(fused_kernel, groups, ranks, per, aminos...  16 us
    pallas_call x1, Pallas kernels, fused(): pl.pallas_call(write_kernel, out_shape=(jax.ShapeDtypeStruct(emb.shape, B...  0.65 us

profile of v5, /device:TPU:0, one launch (start us, length us, event | category | flops | bytes accessed | tf_op | source)
XLA Modules:
  0.0 17.3 jit_solution(8693705516148402069)
XLA Ops:
  0.6 16.0 %shard_map.104 = (bf16[32,4,256]{2,1,0:T(4,128)(2,1)S(1)}, bf16[16,4,128]{2,1,0:T(4,128)(2,1)S(1)}) custom-call(bf16[8,4,4,256]{3,2,1,0:T(4,128)(2,1)} %bitcast.7, s32[4,32]{1,0:T(4,128)} %bitcast.9, s32[1,32]{1,0:T(1,128)} %bitcast.11, bf16[16,4,128]{2,1,0:T(4,128)(2,1)} %pair_hbm.1, bf16[256,1024]{1,0:T(8,128)(2,1)} %proj_hbm.1, bf16[8,128]{1,0:T(8,128)(2,1)} %bitcast.10, ...), custom_call_target="tpu_custom_call" | custom-call | tf_op jit(solution)/shard_map/pallas_call | solution.py:501
  16.7 0.7 %shard_map.105 = (bf16[32,4,256]{2,1,0:T(4,128)(2,1)}, bf16[16,4,128]{2,1,0:T(4,128)(2,1)}) custom-call(bf16[32,4,256]{2,1,0:T(4,128)(2,1)S(1)} %get-tuple-element.4.out_ref, bf16[16,4,128]{2,1,0:T(4,128)(2,1)S(1)} %get-tuple-element.5.pair_ref), custom_call_target="tpu_custom_call" | custom-call | tf_op jit(solution)/shard_map/pallas_call | solution.py:528

commit v6 on v5

--- a/solution.py
+++ b/solution.py
@@ -260,7 +260,8 @@
         others.append((0, group, chip * cores + lax.rem(core + x, cores)))
 
     barrier = pltpu.get_barrier_semaphore()
-    for _, g, r in others:
+    ahead = (groups - 1) * ranks
+    for _, g, r in others[:cores] + others[ahead:ahead + cores] + others[cores:ahead] + others[ahead + cores:]:
         pl.semaphore_signal(
             barrier, inc=1, device_id={"seq": g, "res": r}, device_id_type=pl.DeviceIdType.MESH
         )

time: 17.5 us -> 17.5 us (level)
  no operation moved by 1% of the time
where the time goes in v6:
time: 17.5 us; the launch traced here: 17.3 us
  Pallas kernels  16.7 us (95%)
  between operations  0.64 us (4%)
    pallas_call x1, Pallas kernels, fused(): pl.pallas_call(functools.partial(fused_kernel, groups, ranks, per, aminos...  16 us
    pallas_call x1, Pallas kernels, fused(): pl.pallas_call(write_kernel, out_shape=(jax.ShapeDtypeStruct(emb.shape, B...  0.65 us

profile of v6, /device:TPU:0, one launch (start us, length us, event | category | flops | bytes accessed | tf_op | source)
XLA Modules:
  0.0 17.3 jit_solution(2668072544278477708)
XLA Ops:
  0.6 16.0 %shard_map.104 = (bf16[32,4,256]{2,1,0:T(4,128)(2,1)S(1)}, bf16[16,4,128]{2,1,0:T(4,128)(2,1)S(1)}) custom-call(bf16[8,4,4,256]{3,2,1,0:T(4,128)(2,1)} %bitcast.7, s32[4,32]{1,0:T(4,128)} %bitcast.9, s32[1,32]{1,0:T(1,128)} %bitcast.11, bf16[16,4,128]{2,1,0:T(4,128)(2,1)} %pair_hbm.1, bf16[256,1024]{1,0:T(8,128)(2,1)} %proj_hbm.1, bf16[8,128]{1,0:T(8,128)(2,1)} %bitcast.10, ...), custom_call_target="tpu_custom_call" | custom-call | tf_op jit(solution)/shard_map/pallas_call | solution.py:502
  16.7 0.7 %shard_map.105 = (bf16[32,4,256]{2,1,0:T(4,128)(2,1)}, bf16[16,4,128]{2,1,0:T(4,128)(2,1)}) custom-call(bf16[32,4,256]{2,1,0:T(4,128)(2,1)S(1)} %get-tuple-element.4.out_ref, bf16[16,4,128]{2,1,0:T(4,128)(2,1)S(1)} %get-tuple-element.5.pair_ref), custom_call_target="tpu_custom_call" | custom-call | tf_op jit(solution)/shard_map/pallas_call | solution.py:529
